TPU v7x, 256 devices: a whole 4x4x8 slice. The times are simulated.
256 devices in a mesh: row: 8 (over x, y_lo), col: 32 (over y_hi, z, core).
Axes of the slice: x: 4, y: 4 (y_hi: 2, y_lo: 2; y = y_hi * 2 + y_lo), z: 8, core: 2. Of those that a mesh axis runs over, the one named last changes fastest.
Arguments:
- mlp_param: float32 [6144, 24576], P('row', 'col'), may hold values from -250 to 250
- mlp_grad: bfloat16 [6144, 24576], P('row', 'col'), may hold values from -250 to 250
- mlp_row_state: float32 [6144], P('row'), may hold values from 0.03 to 2.7
- mlp_col_state: float32 [24576], P('col'), may hold values from 0.02 to 0.3
- attn_param: float32 [6144, 6144], P('row', 'col'), may hold values from -250 to 250
- attn_grad: bfloat16 [6144, 6144], P('row', 'col'), may hold values from -250 to 250
- attn_row_state: float32 [6144], P('row'), may hold values from 0.03 to 2.7
- attn_col_state: float32 [6144], P('col'), may hold values from 0.02 to 0.3
Outputs:
- mlp_param_new: float32 [6144, 24576], P('row', 'col')
- attn_param_new: float32 [6144, 6144], P('row', 'col')
- mlp_row_new: float32 [6144], P('row')
- mlp_col_new: float32 [24576], P('col')
- attn_row_new: float32 [6144], P('row')
- attn_col_new: float32 [6144], P('col')
- attn_copy: bfloat16 [6144, 6144], P(None, 'col')
All inputs are finite; a program needn't handle non-finite values.
Results may differ from a plain program's by a relative error of at most 0.0004.
Values may be sent and summed in bfloat16 or wider, within the bound.
No kernel may reach another device: no remote copies, remote signals or barrier semaphores. Data moves between devices by JAX's collectives and lax.ppermute only.
A program may use at most 64 MiB of HBM per device.

v0:
```python
import functools

import jax
import jax.numpy as jnp
from jax import lax
from jax.experimental import pallas as pl
from jax.experimental.pallas import tpu as pltpu
from jax.sharding import Mesh
from jax.sharding import PartitionSpec as P

STEP = 4
ROW = ("row_0", "row_1")
COL = ("col_0", "col_1", "col_2")
Y_HI, Z, CORE = COL
LAYERS = (Y_HI, Z)

TINY_SQUARE = 1e-30
LEARN_RATE = 0.05
DECAY_POWER = 0.8
KEEP = 1.0 - STEP ** (-DECAY_POWER)

F32, BF16 = jnp.float32, jnp.bfloat16
SLAB = 16
LANES = 128
ON_CHIP = pl.BlockSpec(memory_space=pltpu.VMEM)
OFF_CHIP = pl.BlockSpec(memory_space=pltpu.HBM)


def call(kernel, outs, args, in_specs=None, out_specs=None, scratch=(), limit=4 << 20, aliases=None, flops=0):
    return pl.pallas_call(
        kernel,
        out_shape=outs,
        in_specs=in_specs or [ON_CHIP] * len(args),
        out_specs=out_specs or [ON_CHIP] * len(outs),
        scratch_shapes=scratch,
        input_output_aliases=aliases or {},
        cost_estimate=pl.CostEstimate(flops=flops, bytes_accessed=flops, transcendentals=0) if flops else None,
        compiler_params=pltpu.CompilerParams(vmem_limit_bytes=limit),
    )(*args)


def tiles(value):
    width = value.shape[1] // LANES
    return sum((value[:, k * LANES : (k + 1) * LANES] for k in range(1, width)), value[:, :LANES])


def wide(value, width):
    return jnp.concatenate([value] * (width // LANES), axis=1)


def turned_sum(ref, start):
    return jnp.sum(ref[pl.ds(start, LANES), :].T, axis=0, keepdims=True)


def down(value):
    return jnp.broadcast_to(value, (LANES, LANES)).T


def fold(value):
    return value[:8] + value[8:]


def added(ref):
    total = ref[0]
    for k in range(1, ref.shape[0]):
        total = total + ref[k]
    return total


def sums_kernel(
    g_hbm, ga_hbm, p_hbm, pa_hbm, sent_ref, rows_ref, psum_ref, g_ref, ga_ref, p_ref, pa_ref, lane_ref, sems
):
    rows, cols = g_hbm.shape
    attn_cols = ga_hbm.shape[0]
    blocks = rows // LANES
    g_copies = [
        pltpu.make_async_copy(g_hbm.at[pl.ds(b * LANES, LANES)], g_ref.at[pl.ds(b * LANES, LANES)], sems.at[b])
        for b in range(blocks)
    ]
    p_copies = [
        pltpu.make_async_copy(
            p_hbm.at[pl.ds(b * LANES, LANES)], p_ref.at[pl.ds(b * LANES, LANES)], sems.at[blocks + b]
        )
        for b in range(blocks)
    ]
    ga_copy = pltpu.make_async_copy(ga_hbm, ga_ref, sems.at[2 * blocks])
    pa_copy = pltpu.make_async_copy(pa_hbm, pa_ref, sems.at[2 * blocks + 1])
    for copy in (*g_copies, ga_copy, *p_copies, pa_copy):
        copy.start()
    lane_ref[pl.ds(rows, 2 * LANES), :] = jnp.zeros((2 * LANES, LANES), F32)

    def squares(ref, start, first):
        def step(s, acc):
            g = ref[pl.ds(start + s * SLAB, SLAB), :].astype(F32)
            g = g * g
            lane_ref[pl.ds(first + start + s * SLAB, SLAB), :] = tiles(g)
            return acc + fold(g)

        return step

    def own_squares(ref, start):
        def step(s, acc):
            p = ref[pl.ds(start + s * SLAB, SLAB), :]
            return acc + fold(p * p)

        return step

    eight = jnp.zeros((8, cols), F32)
    steps = LANES // SLAB
    col_sum = eight
    for b, copy in enumerate(g_copies):
        copy.wait()
        col_sum = lax.fori_loop(0, steps, squares(g_ref, b * LANES, 0), col_sum, unroll=True)
        rows_ref[:, pl.ds(b * LANES, LANES)] = turned_sum(lane_ref, b * LANES)
    ga_copy.wait()
    row_sum = lax.fori_loop(0, attn_cols // SLAB, squares(ga_ref, 0, rows), jnp.zeros((8, rows), F32), unroll=4)
    rows_ref[:, pl.ds(rows, rows)] = jnp.sum(row_sum, axis=0, keepdims=True)
    rows_ref[...] += jnp.concatenate(
        [jnp.full((1, rows), cols * TINY_SQUARE, F32), jnp.full((1, rows), attn_cols * TINY_SQUARE, F32)], axis=1
    )
    col_sums = jnp.concatenate(
        [
            jnp.sum(col_sum, axis=0, keepdims=True),
            turned_sum(lane_ref, rows),
            turned_sum(lane_ref, rows + LANES),
        ],
        axis=1,
    ) + rows * TINY_SQUARE
    for k in range(sent_ref.shape[0]):
        sent_ref[k] = col_sums
    p_sum = eight
    for b, copy in enumerate(p_copies):
        copy.wait()
        p_sum = lax.fori_loop(0, steps, own_squares(p_ref, b * LANES), p_sum, unroll=True)
    pa_copy.wait()
    pa_sum = lax.fori_loop(0, attn_cols // SLAB, own_squares(pa_ref, 0), jnp.zeros((8, rows), F32), unroll=4)
    psum_ref[:, :LANES] = jnp.sum(tiles(p_sum), axis=0, keepdims=True)
    psum_ref[:, LANES:] = jnp.sum(tiles(pa_sum), axis=0, keepdims=True)


def columns_kernel(
    rows_total, got_ref, rows_ref, g_ref, ga_ref, pa_ref, state_ref, attn_state_ref,
    cols_ref, attn_cols_ref, kept_ref, sent_ref, early_ref, lane_ref,
):
    rows, cols = g_ref.shape
    attn_cols = ga_ref.shape[0]
    half = rows // 2
    core = lax.axis_index(CORE)
    total = added(got_ref)
    row_sums = rows_ref[...]
    cols_new = KEEP * state_ref[...].reshape(1, cols) + (1.0 - KEEP) * (total[:, :cols] / rows_total)
    cols_ref[...] = cols_new.reshape(cols)
    attn_state = attn_state_ref[...].reshape(1, attn_cols)
    attn_new = KEEP * attn_state + (1.0 - KEEP) * (total[:, cols : cols + attn_cols] / rows_total)
    attn_cols_ref[...] = attn_new.reshape(attn_cols)
    inverse = jnp.broadcast_to(1.0 / cols_new, (SLAB, cols))
    attn_inverse = jnp.concatenate([1.0 / attn_new, jnp.ones((1, 2 * LANES - attn_cols), F32)], axis=1)
    down_inverse = [down(attn_inverse[:, k * LANES : (k + 1) * LANES]) for k in range(2)]

    def step(s, carry):
        g = g_ref[pl.ds(s * SLAB, SLAB), :].astype(F32)
        lane_ref[pl.ds(s * SLAB, SLAB), :] = tiles(g * g * inverse)
        return carry

    lax.fori_loop(0, rows // SLAB, step, 0, unroll=8)
    w_attn = jnp.zeros((8, rows), F32)
    for s in range(attn_cols // SLAB):
        g = ga_ref[pl.ds(s * SLAB, SLAB), :].astype(F32)
        at = s * SLAB
        scale = down_inverse[at // LANES][at % LANES : at % LANES + SLAB]
        w_attn = w_attn + fold(g * g * wide(scale, rows))
    w_attn = jnp.sum(w_attn, axis=0, keepdims=True)
    w_mlp = jnp.concatenate([turned_sum(lane_ref, b * LANES) for b in range(rows // LANES)], axis=1)
    vectors = (row_sums[:, :rows], row_sums[:, rows:], w_mlp, w_attn)
    first = jnp.concatenate([v[:, :half] for v in vectors], axis=1)
    last = jnp.concatenate([v[:, half:] for v in vectors], axis=1)
    early = early_ref.shape[0] // 3
    for at in range(0, early, SLAB):
        p = pa_ref[pl.ds(at, SLAB), :]
        high = p.astype(BF16)
        early_ref[pl.ds(at, SLAB), :] = high
        early_ref[pl.ds(early + at, SLAB), :] = (p - high.astype(F32)).astype(BF16)
    early_ref[pl.ds(2 * early, early), :] = ga_ref[pl.ds(0, early), :]
    kept_ref[...] = jnp.where(core == 0, first, last)
    sent_ref[...] = jnp.where(core == 0, last, first)


def spread_kernel(kept_ref, got_ref, psum_ref, sent_ref):
    value = jnp.concatenate([kept_ref[...] + got_ref[...], psum_ref[...]], axis=1)
    for k in range(sent_ref.shape[0]):
        sent_ref[k] = value


def rows_kernel(widths, got_ref, state_ref, attn_state_ref, sent_ref):
    rows = state_ref.shape[0]
    half = rows // 2
    core = lax.axis_index(CORE)
    total = added(got_ref)
    new, parts = [], []
    for k, (ref, width) in enumerate(zip((state_ref, attn_state_ref), widths)):
        state = ref[...].reshape(1, rows)
        state = jnp.where(core == 0, state[:, :half], state[:, half:])
        new.append(KEEP * state + (1.0 - KEEP) * (total[:, k * half : (k + 1) * half] / width))
        parts.append(tiles(total[:, (2 + k) * half : (3 + k) * half] / new[k]))
    value = jnp.concatenate([*parts, total[:, 4 * half :], *new], axis=1)
    for k in range(sent_ref.shape[0]):
        sent_ref[k] = value


def factor(got_ref, matrix, count):
    total = got_ref[0, :, : 4 * LANES]
    for k in range(1, got_ref.shape[0]):
        total = total + got_ref[k, :, : 4 * LANES]
    q, p = (
        jnp.broadcast_to(jnp.sum(total[:, k * LANES : (k + 1) * LANES], axis=1, keepdims=True), (1, LANES))
        for k in (matrix, 2 + matrix)
    )
    return LEARN_RATE * jnp.sqrt(p / count) / jnp.maximum(1.0, jnp.sqrt(q / count))


def new_rows(got_ref, matrix, half, dx=0):
    row = place(dx, 0)
    at = pl.ds(4 * LANES + matrix * half, half)
    return jnp.concatenate([got_ref[2 * row, :, at], got_ref[2 * row + 1, :, at]], axis=1)


def attn_scales(count, got_ref, attn_cols_ref):
    attn_cols = attn_cols_ref.shape[0]
    across = attn_cols_ref[...].reshape(1, attn_cols)
    across = lax.rsqrt(jnp.concatenate([across, jnp.ones((1, 2 * LANES - attn_cols), F32)], axis=1))
    scale = factor(got_ref, 1, count)
    return [down(across[:, k * LANES : (k + 1) * LANES] * scale) for k in range(2)]


def attn_new(g, p, at, across, along):
    scale = across[at // LANES][at % LANES : at % LANES + SLAB]
    return p - g * wide(scale, g.shape[1]) * along


def attn_kernel(count, got_ref, attn_cols_ref, ga_ref, pa_ref, attn_ref, block_ref, rest_ref):
    attn_cols, rows = ga_ref.shape
    early = attn_cols - rest_ref.shape[0]
    across = attn_scales(count, got_ref, attn_cols_ref)
    along = jnp.broadcast_to(lax.rsqrt(new_rows(got_ref, 1, rows // 2)), (SLAB, rows))
    for at in range(0, attn_cols, SLAB):
        rows_at = pl.ds(at, SLAB)
        value = attn_new(ga_ref[rows_at, :].astype(F32), pa_ref[rows_at, :], at, across, along)
        attn_ref[pl.ds(at, SLAB), :] = value
        block_ref[pl.ds(at, SLAB), :] = value.astype(BF16)
        if at >= early:
            rest_ref[pl.ds(at - early, SLAB), :] = value.astype(BF16)


def early_kernel(count, got_ref, attn_cols_ref, ahead_ref, out_ref):
    early, rows = out_ref.shape
    across = attn_scales(count, got_ref, attn_cols_ref)
    along = jnp.broadcast_to(lax.rsqrt(new_rows(got_ref, 1, rows // 2, 2)), (SLAB, rows))
    for at in range(0, early, SLAB):
        high, low, g = (ahead_ref[pl.ds(k * early + at, SLAB), :].astype(F32) for k in range(3))
        out_ref[pl.ds(at, SLAB), :] = attn_new(g, high + low, at, across, along).astype(BF16)


def place(dx, dy):
    x = lax.rem(lax.axis_index("row_0") + dx, lax.axis_size("row_0"))
    y = lax.rem(lax.axis_index("row_1") + dy, lax.axis_size("row_1"))
    return x * lax.axis_size("row_1") + y


def fill_kernel(offsets, *refs):
    blocks, out_hbm, sems = refs[: len(offsets)], refs[-2], refs[-1]
    width = blocks[0].shape[1]
    copies = []
    for k, (ref, offset) in enumerate(zip(blocks, offsets)):
        dx, dy, first = offset
        at = pl.multiple_of(place(dx, dy) * width, width)
        target = out_hbm.at[pl.ds(first, ref.shape[0]), pl.ds(at, width)]
        copies.append(pltpu.make_async_copy(ref, target, sems.at[k]))
        copies[-1].start()
    for copy in copies:
        copy.wait()


def fill(copy, offsets, blocks):
    count = len(blocks)
    return call(
        functools.partial(fill_kernel, offsets),
        [jax.ShapeDtypeStruct(copy.shape, copy.dtype)],
        (*blocks, copy),
        in_specs=[ON_CHIP] * count + [OFF_CHIP],
        out_specs=[OFF_CHIP],
        scratch=[pltpu.SemaphoreType.DMA((count,))],
        aliases={count: 0},
    )[0]


def finish_kernel(
    count, block_ref, got_ref, cols_ref, attn_cols_ref, attn_ref, g_ref, p_ref,
    copy_hbm, attn_hbm, new_hbm, rows_hbm, cols_hbm, attn_rows_hbm, attn_cols_hbm,
    new_ref, rows_ref, attn_rows_ref, sems,
):
    rows, cols = g_ref.shape
    blocks = rows // LANES
    copies = []

    def put(source, target):
        copies.append(pltpu.make_async_copy(source, target, sems.at[len(copies)]))
        copies[-1].start()

    put(block_ref, copy_hbm.at[:, pl.ds(pl.multiple_of(place(0, 0) * rows, rows), rows)])
    put(attn_ref, attn_hbm)
    put(cols_ref, cols_hbm)
    put(attn_cols_ref, attn_cols_hbm)
    row_factors = new_rows(got_ref, 0, rows // 2)
    rows_ref[...] = row_factors.reshape(rows)
    attn_rows_ref[...] = new_rows(got_ref, 1, rows // 2).reshape(rows)
    along = jnp.broadcast_to(lax.rsqrt(cols_ref[...].reshape(1, cols)), (SLAB, cols))
    scale = factor(got_ref, 0, count)
    row_scale = lax.rsqrt(row_factors)
    for b in range(blocks):
        across = down(row_scale[:, b * LANES : (b + 1) * LANES] * scale)
        for s in range(LANES // SLAB):
            at = pl.ds(b * LANES + s * SLAB, SLAB)
            new_ref[at, :] = (
                p_ref[at, :] - g_ref[at, :].astype(F32) * wide(across[s * SLAB : (s + 1) * SLAB], cols) * along
            )
        at = pl.ds(b * LANES, LANES)
        put(new_ref.at[at], new_hbm.at[at])
    put(rows_ref, rows_hbm)
    put(attn_rows_ref, attn_rows_hbm)
    for copy in copies:
        copy.wait()


def everyone(value, axes):
    return lax.all_to_all(value, axes, 0, 0, tiled=True)


def moved(value, dx, dy):
    xs, ys = lax.axis_size("row_0"), lax.axis_size("row_1")
    pairs = [(x * ys + y, (x + dx) % xs * ys + (y + dy) % ys) for x in range(xs) for y in range(ys)]
    return lax.ppermute(value, ROW, pairs)


def other_core(value):
    return lax.ppermute(value, CORE, [(0, 1), (1, 0)])


def step(
    mlp_param,
    mlp_grad,
    mlp_row_state,
    mlp_col_state,
    attn_param,
    attn_grad,
    attn_row_state,
    attn_col_state,
):
    rows, cols = mlp_grad.shape
    attn_cols = attn_grad.shape[1]
    half = rows // 2
    row_devices, layers = lax.axis_size(ROW), lax.axis_size(LAYERS)
    message = -(-(cols + attn_cols) // LANES) * LANES
    rows_total = rows * row_devices
    widths = (float(cols * lax.axis_size(COL)), float(attn_cols * lax.axis_size(COL)))
    counts = (rows_total * widths[0], rows_total * widths[1])
    attn_grad, attn_param = attn_grad.T, attn_param.T
    blocks = rows // LANES
    early = attn_cols // 2 // SLAB * SLAB

    sent, row_sums, p_sums, g, ga, p, pa = call(
        sums_kernel,
        [
            pltpu.VMEM((row_devices, 1, message), F32),
            pltpu.VMEM((1, 2 * rows), F32),
            pltpu.VMEM((1, 2 * LANES), F32),
            pltpu.VMEM((rows, cols), BF16),
            pltpu.VMEM((attn_cols, rows), BF16),
            pltpu.VMEM((rows, cols), F32),
            pltpu.VMEM((attn_cols, rows), F32),
        ],
        (mlp_grad, attn_grad, mlp_param, attn_param),
        in_specs=[OFF_CHIP] * 4,
        scratch=[
            pltpu.VMEM((rows + 2 * LANES, LANES), F32),
            pltpu.SemaphoreType.DMA((2 * blocks + 2,)),
        ],
        limit=119 << 19,
    )
    got = everyone(sent, ROW)
    cols_new, attn_cols_new, kept, sent, ahead = call(
        functools.partial(columns_kernel, float(rows_total)),
        [
            pltpu.VMEM((cols,), F32),
            pltpu.VMEM((attn_cols,), F32),
            pltpu.VMEM((1, 4 * half), F32),
            pltpu.VMEM((1, 4 * half), F32),
            pltpu.VMEM((3 * early, rows), BF16),
        ],
        (got, row_sums, g, ga, pa, mlp_col_state, attn_col_state),
        scratch=[pltpu.VMEM((rows, LANES), F32)],
    )
    swapped = other_core(sent)
    (sent,) = call(
        spread_kernel,
        [pltpu.VMEM((layers, 1, 4 * half + 2 * LANES), F32)],
        (kept, swapped, p_sums),
    )
    got = everyone(sent, LAYERS)
    (sent,) = call(
        functools.partial(rows_kernel, widths),
        [pltpu.VMEM((2 * row_devices, 1, 4 * LANES + 2 * half), F32)],
        (got, mlp_row_state, attn_row_state),
    )
    got = everyone(sent, (*ROW, CORE))
    ahead = moved(ahead, 2, 0)
    attn_new, block, rest = call(
        functools.partial(attn_kernel, counts[1]),
        [
            pltpu.VMEM((attn_cols, rows), F32),
            pltpu.VMEM((attn_cols, rows), BF16),
            pltpu.VMEM((attn_cols - early, rows), BF16),
        ],
        (got, attn_cols_new, ga, pa),
    )
    (first_across,) = call(
        functools.partial(early_kernel, counts[1]),
        [pltpu.VMEM((early, rows), BF16)],
        (got, attn_cols_new, ahead),
    )
    across = moved(rest, 2, 0)
    partner = moved(block, 0, 1)
    left, right = moved(block, 1, 0), moved(block, 3, 0)
    partner_first = moved(first_across, 0, 1)
    partner_across = moved(across, 0, 1)
    partner_left = moved(partner, 1, 0)
    partner_right = moved(partner, 3, 0)
    copy, attn_new, mlp_new, rows_new, cols_new, attn_rows_new, attn_cols_new = call(
        functools.partial(finish_kernel, counts[0]),
        [
            jax.ShapeDtypeStruct((attn_cols, rows_total), BF16),
            jax.ShapeDtypeStruct((attn_cols, rows), F32),
            jax.ShapeDtypeStruct((rows, cols), F32),
            jax.ShapeDtypeStruct((rows,), F32),
            jax.ShapeDtypeStruct((cols,), F32),
            jax.ShapeDtypeStruct((rows,), F32),
            jax.ShapeDtypeStruct((attn_cols,), F32),
        ],
        (block, got, cols_new, attn_cols_new, attn_new, g, p),
        out_specs=[OFF_CHIP] * 7,
        scratch=[
            pltpu.VMEM((rows, cols), F32),
            pltpu.VMEM((rows,), F32),
            pltpu.VMEM((rows,), F32),
            pltpu.SemaphoreType.DMA((blocks + 6,)),
        ],
        flops=1 << 22,
    )
    copy = fill(
        copy,
        ((2, 0, 0), (2, 0, early), (0, 1, 0), (3, 0, 0), (1, 0, 0)),
        (first_across, across, partner, left, right),
    )
    copy = fill(
        copy,
        ((2, 1, 0), (2, 1, early), (3, 1, 0), (1, 1, 0)),
        (partner_first, partner_across, partner_left, partner_right),
    )
    return mlp_new, attn_new.T, rows_new, cols_new, attn_rows_new, attn_cols_new, copy.T


def solution(mesh):
    finer = Mesh(mesh.devices.reshape(4, 2, 2, 8, 2), (*ROW, *COL))
    return jax.shard_map(
        step,
        mesh=finer,
        in_specs=(
            P(ROW, COL),
            P(ROW, COL),
            P(ROW),
            P(COL),
            P(ROW, COL),
            P(ROW, COL),
            P(ROW),
            P(COL),
        ),
        out_specs=(P(ROW, COL), P(ROW, COL), P(ROW), P(COL), P(ROW), P(COL), P(None, COL)),
        check_vma=False,
    )
```

profile of v0, /device:TPU:1, one launch (start us, length us, event | category | flops | bytes accessed | tf_op | source)
XLA Modules:
  0.0 72.4 jit_solution(15509187765717452184)
XLA Ops:
  0.7 2.5 %shard_map.135 = (f32[8,1,1024]{2,1,0:T(1,128)S(1)}, f32[1,1536]{1,0:T(1,128)S(1)}, f32[1,256]{1,0:T(1,128)S(1)}, bf16[768,768]{1,0:T(8,128)(2,1)S(1)}, bf16[192...) custom-call(bf16[768,768]{1,0:T(8,128)(2,1)} %g_hbm.1, bf16[192,768]{1,0:T(8,128)(2,1)} %bitcast.6, ...), custom_call_target="tpu_custom_call" | custom-call | tf_op jit(solution)/shard_map/pallas_call | solution.py:30
  3.2 0.0 copy-start.2
  3.2 1.4 %copy-done.2 = f32[768,768]{1,0:T(8,128)} copy-done((f32[768,768]{1,0:T(8,128)}, f32[768,768]{1,0:T(8,128)S(1)}, u32[]{:S(2)}) %copy-start.2) | copy-done | bytes 2359320
  4.6 10.9 %all_to_all.15.got_ref = f32[8,1,1024]{2,1,0:T(1,128)S(1)} all-to-all(f32[8,1,1024]{2,1,0:T(1,128)S(1)} %get-tuple-element.29), channel_id=1, replica_groups=mesh['row_0'=4,'row_1'=2,'col_0'=2,'col_1'=8,'col_2'=2] {'row_0','row_1'}, dimensions={0} | all-to-all | bytes 65536 | tf_op jit(solution)/shard_map/all_to_all | solution.py:335
  15.5 0.7 shard_map.136
  16.2 0.0 copy-start
  16.2 1.0 %copy-done = bf16[768,768]{1,0:T(8,128)(2,1)} copy-done((bf16[768,768]{1,0:T(8,128)(2,1)}, bf16[768,768]{1,0:T(8,128)(2,1)S(1)}, u32[]{:S(2)}) %copy-start) | copy-done | bytes 1179672
  17.2 2.1 %collective-permute-start = (f32[1,1536]{1,0:T(1,128)S(1)}, f32[1,1536]{1,0:T(1,128)S(1)}, u32[]{:S(2)}, u32[]{:S(2)}) collective-permute-start(f32[1,1536]{1,0:T(1,128)S(1)} %get-tuple-element.35), channel_id=1, source_target_pairs={{0,1},{1,0},{2,3},{3,2},{4,5},{5,4},{6,7},{7,6},{8,9},{9,8},{10,11... | collective-permute-start | bytes 18440 | tf_op jit(solution)/shard_map/ppermute | solution.py:345
  19.3 0.8 %collective-permute-done.got_ref = f32[1,1536]{1,0:T(1,128)S(1)} collective-permute-done((f32[1,1536]{1,0:T(1,128)S(1)}, f32[1,1536]{1,0:T(1,128)S(1)}, u32[]{:S(2)}, u32[]{:S(2)}) %collective-permute-start) | collective-permute-done | bytes 6176 | tf_op jit(solution)/shard_map/ppermute | solution.py:345
  20.1 0.7 shard_map.137
  20.7 10.6 %all-to-all-start.1 = ((f32[16,1,1792]{2,1,0:T(1,128)}), f32[16,1,1792]{2,1,0:T(1,128)S(1)}, u32[]{:S(2)}, u32[]{:S(2)}) async-start(f32[16,1,1792]{2,1,0:T(1,128)} %shard_map.137), calls=%async_computation.1 | async-start | bytes 229376 | tf_op jit(solution)/shard_map/all_to_all | solution.py:335
  31.4 1.1 %collective-permute-start.1 = (bf16[288,768]{1,0:T(8,128)(2,1)S(1)}, bf16[288,768]{1,0:T(8,128)(2,1)S(1)}, u32[]{:S(2)}, u32[]{:S(2)}) collective-permute-start(bf16[288,768]{1,0:T(8,128)(2,1)S(1)} %get-tuple-element.48), channel_id=1, source_target_pairs={{0,128},{32,160},{64,192},{96,224},{128,0},{160,32},{192,64},{224,... | collective-permute-start | bytes 1327112 | tf_op jit(solution)/shard_map/ppermute | solution.py:341
  32.4 7.9 %all-to-all-done.1.got_ref = f32[16,1,1792]{2,1,0:T(1,128)S(1)} async-done(((f32[16,1,1792]{2,1,0:T(1,128)}), f32[16,1,1792]{2,1,0:T(1,128)S(1)}, u32[]{:S(2)}, u32[]{:S(2)}) %all-to-all-start.1) | async-done | bytes 114720 | tf_op jit(solution)/shard_map/all_to_all | solution.py:335
  40.3 10.3 %all_to_all.16.got_ref = f32[16,1,1280]{2,1,0:T(1,128)S(1)} all-to-all(f32[16,1,1280]{2,1,0:T(1,128)S(1)} %shard_map.138), channel_id=1, replica_groups=mesh['row_0'=4,'row_1'=2,'col_0'=2,'col_1'=8,'col_2'=2] {'row_0','row_1'..., dimensions={0} | all-to-all | bytes 163840 | tf_op jit(solution)/shard_map/all_to_all | solution.py:335
  50.6 1.0 %copy-done.5 = bf16[192,768]{1,0:T(8,128)(2,1)S(1)} copy-done((bf16[192,768]{1,0:T(8,128)(2,1)S(1)}, bf16[192,768]{1,0:T(8,128)(2,1)}, u32[]{:S(2)}) %copy-start.5) | copy-done | bytes 294936
  51.6 0.3 shard_map.139
  51.9 0.5 collective-permute-start.5
  52.3 0.2 collective-permute-start.8
  52.5 2.5 %collective-permute-start.9 = (bf16[192,768]{1,0:T(8,128)(2,1)S(1)}, bf16[192,768]{1,0:T(8,128)(2,1)S(1)}, u32[]{:S(2)}, u32[]{:S(2)}) collective-permute-start(bf16[192,768]{1,0:T(8,128)(2,1)S(1)} %get-tuple-element.38.block_ref), channel_id=1, source_target_pairs={{0,192},{32,224},{64,0},{96,32},{128,64},{160,96},{192,128},{224,1... | collective-permute-start | bytes 884744 | tf_op jit(solution)/shard_map/ppermute | solution.py:341
  55.0 0.0 collective-permute-start.3
  55.0 5.1 %collective-permute-done.5.refs_2_ = bf16[192,768]{1,0:T(8,128)(2,1)S(1)} collective-permute-done((bf16[192,768]{1,0:T(8,128)(2,1)S(1)}, bf16[192,768]{1,0:T(8,128)(2,1)S(1)}, u32[]{:S(2)}, u32[]{:S(2)}) %collective-permute-start.5) | collective-permute-done | bytes 294944 | tf_op jit(solution)/shard_map/ppermute | solution.py:341
  60.1 0.3 collective-permute-start.6
  60.4 2.4 %collective-permute-start.7 = (bf16[192,768]{1,0:T(8,128)(2,1)S(1)}, bf16[192,768]{1,0:T(8,128)(2,1)S(1)}, u32[]{:S(2)}, u32[]{:S(2)}) collective-permute-start(bf16[192,768]{1,0:T(8,128)(2,1)S(1)} %collective-permute-done.5.refs_2_), channel_id=1, source_target_pairs={{0,192},{32,224},{64,0},{96,32},{128,64},{160,96},{192,128},{224,1... | collective-permute-start | bytes 884744 | tf_op jit(solution)/shard_map/ppermute | solution.py:341
  62.8 0.2 shard_map.141.refs_0_
  63.0 0.8 %collective-permute-done.3.refs_1_ = bf16[96,768]{1,0:T(8,128)(2,1)S(1)} collective-permute-done((bf16[96,768]{1,0:T(8,128)(2,1)S(1)}, bf16[96,768]{1,0:T(8,128)(2,1)S(1)}, u32[]{:S(2)}, u32[]{:S(2)}) %collective-permute-start.3) | collective-permute-done | bytes 147488 | tf_op jit(solution)/shard_map/ppermute | solution.py:341
  63.9 1.1 %collective-permute-start.2 = (bf16[96,768]{1,0:T(8,128)(2,1)S(1)}, bf16[96,768]{1,0:T(8,128)(2,1)S(1)}, u32[]{:S(2)}, u32[]{:S(2)}) collective-permute-start(bf16[96,768]{1,0:T(8,128)(2,1)S(1)} %shard_map.141.refs_0_), channel_id=1, source_target_pairs={{0,32},{32,0},{64,96},{96,64},{128,160},{160,128},{192,224},{224,1... | collective-permute-start | bytes 442376 | tf_op jit(solution)/shard_map/ppermute | solution.py:341
  65.0 0.3 collective-permute-start.4
  65.3 1.7 %copy-done.3 = f32[768,768]{1,0:T(8,128)S(1)} copy-done((f32[768,768]{1,0:T(8,128)S(1)}, f32[768,768]{1,0:T(8,128)}, u32[]{:S(2)}) %copy-start.3) | copy-done | bytes 2359320
  67.0 1.8 %shard_map.140 = (bf16[192,6144]{1,0:T(8,128)(2,1)}, f32[192,768]{1,0:T(8,128)}, f32[768,768]{1,0:T(8,128)}, f32[768]{0:T(1024)}, f32[768]{0:T(1024)}, /*index=5*/f32[768]{0:T(1024)}, f32[192]{0:T(256)}) custom-call(bf16[192,768]{1,0:T(8,128)(2,1)S(1)} %get-tuple-element.38.block_ref, f32[16,1,1280]{2,1,0:T(1,128)S(1)} %all_to_all.16.got_ref, ...), custom_call_target="tpu_custom_call" | custom-call | flops 4194304 | bytes 4194304 | tf_op jit(solution)/shard_map/pallas_call | solution.py:30
  68.8 1.1 %shard_map.142.refs_4_ = bf16[192,6144]{1,0:T(8,128)(2,1)} custom-call(bf16[96,768]{1,0:T(8,128)(2,1)S(1)} %shard_map.141.refs_0_, bf16[96,768]{1,0:T(8,128)(2,1)S(1)} %collective-permute-done.3.refs_1_, bf16[192,768]{1,0:T(8,128)(2,1)S(1)} %collective-permute-done.5.refs_2_, ...), custom_call_target="tpu_custom_call", output_to_operand_aliasing={{}: (5, {})} | custom-call | tf_op jit(solution)/shard_map/pallas_call | solution.py:30
  69.9 1.5 %collective-permute-done.6.refs_2_ = bf16[192,768]{1,0:T(8,128)(2,1)S(1)} collective-permute-done((bf16[192,768]{1,0:T(8,128)(2,1)S(1)}, bf16[192,768]{1,0:T(8,128)(2,1)S(1)}, u32[]{:S(2)}, u32[]{:S(2)}) %collective-permute-start.6) | collective-permute-done | bytes 294944 | tf_op jit(solution)/shard_map/ppermute | solution.py:341
  71.4 0.9 %shard_map.143 = bf16[192,6144]{1,0:T(8,128)(2,1)} custom-call(bf16[96,768]{1,0:T(8,128)(2,1)S(1)} %collective-permute-done.2.refs_0_, bf16[96,768]{1,0:T(8,128)(2,1)S(1)} %collective-permute-done.4.refs_1_, bf16[192,768]{1,0:T(8,128)(2,1)S(1)} %collective-permute-done.6.refs_2_, ...), custom_call_target="tpu_custom_call", output_to_operand_aliasing={{}: (4, {})} | custom-call | tf_op jit(solution)/shard_map/pallas_call | solution.py:30
  (21 shorter events, 0.1 us)
Async XLA Ops:
  0.6 14.8 %copy-start.6 = (f32[768]{0:T(1024)S(1)}, f32[768]{0:T(1024)}, u32[]{:S(2)}) copy-start(f32[768]{0:T(1024)} %state_ref.2) | copy-start | bytes 9220
  0.6 14.8 %copy-start.9 = (f32[192]{0:T(256)S(1)}, f32[192]{0:T(256)}, u32[]{:S(2)}) copy-start(f32[192]{0:T(256)} %attn_state_ref.2) | copy-start | bytes 2308
  3.2 1.4 %copy-start.2 = (f32[768,768]{1,0:T(8,128)}, f32[768,768]{1,0:T(8,128)S(1)}, u32[]{:S(2)}) copy-start(f32[768,768]{1,0:T(8,128)S(1)} %get-tuple-element.41.p_ref) | copy-start | bytes 7077892
  4.6 11.6 %copy-start.4 = (bf16[192,768]{1,0:T(8,128)(2,1)}, bf16[192,768]{1,0:T(8,128)(2,1)S(1)}, u32[]{:S(2)}) copy-start(bf16[192,768]{1,0:T(8,128)(2,1)S(1)} %get-tuple-element.32.ga_ref) | copy-start | bytes 884740
  4.6 35.7 %copy-start.7 = (f32[768]{0:T(1024)S(1)}, f32[768]{0:T(1024)}, u32[]{:S(2)}) copy-start(f32[768]{0:T(1024)} %state_ref.3) | copy-start | bytes 9220
  4.6 35.7 %copy-start.8 = (f32[768]{0:T(1024)S(1)}, f32[768]{0:T(1024)}, u32[]{:S(2)}) copy-start(f32[768]{0:T(1024)} %attn_state_ref.3) | copy-start | bytes 9220
  16.2 1.0 %copy-start = (bf16[768,768]{1,0:T(8,128)(2,1)}, bf16[768,768]{1,0:T(8,128)(2,1)S(1)}, u32[]{:S(2)}) copy-start(bf16[768,768]{1,0:T(8,128)(2,1)S(1)} %get-tuple-element.31.g_ref) | copy-start | bytes 3538948
  17.2 48.1 %copy-start.1 = (bf16[768,768]{1,0:T(8,128)(2,1)S(1)}, bf16[768,768]{1,0:T(8,128)(2,1)}, u32[]{:S(2)}) copy-start(bf16[768,768]{1,0:T(8,128)(2,1)} %copy-done) | copy-start | bytes 3538948
  17.2 2.9 %collective-permute-start = (f32[1,1536]{1,0:T(1,128)S(1)}, f32[1,1536]{1,0:T(1,128)S(1)}, u32[]{:S(2)}, u32[]{:S(2)}) collective-permute-start(f32[1,1536]{1,0:T(1,128)S(1)} %get-tuple-element.35), channel_id=1, source_target_pairs={{0,1},{1,0},{2,3},{3,2},{4,5},{5,4},{6,7},{7,6},{8,9},{9,8},{10,11... | collective-permute-start | bytes 18440 | tf_op jit(solution)/shard_map/ppermute | solution.py:345
  20.7 19.6 %all-to-all-start.1 = ((f32[16,1,1792]{2,1,0:T(1,128)}), f32[16,1,1792]{2,1,0:T(1,128)S(1)}, u32[]{:S(2)}, u32[]{:S(2)}) async-start(f32[16,1,1792]{2,1,0:T(1,128)} %shard_map.137), calls=%async_computation.1 | async-start | bytes 229376 | tf_op jit(solution)/shard_map/all_to_all | solution.py:335
  31.4 29.0 %collective-permute-start.1 = (bf16[288,768]{1,0:T(8,128)(2,1)S(1)}, bf16[288,768]{1,0:T(8,128)(2,1)S(1)}, u32[]{:S(2)}, u32[]{:S(2)}) collective-permute-start(bf16[288,768]{1,0:T(8,128)(2,1)S(1)} %get-tuple-element.48), channel_id=1, source_target_pairs={{0,128},{32,160},{64,192},{96,224},{128,0},{160,32},{192,64},{224,... | collective-permute-start | bytes 1327112 | tf_op jit(solution)/shard_map/ppermute | solution.py:341
  50.6 1.0 %copy-start.5 = (bf16[192,768]{1,0:T(8,128)(2,1)S(1)}, bf16[192,768]{1,0:T(8,128)(2,1)}, u32[]{:S(2)}) copy-start(bf16[192,768]{1,0:T(8,128)(2,1)} %copy-done.4) | copy-start | bytes 884740
  51.9 8.3 %collective-permute-start.5 = (bf16[192,768]{1,0:T(8,128)(2,1)S(1)}, bf16[192,768]{1,0:T(8,128)(2,1)S(1)}, u32[]{:S(2)}, u32[]{:S(2)}) collective-permute-start(bf16[192,768]{1,0:T(8,128)(2,1)S(1)} %get-tuple-element.38.block_ref), channel_id=1, source_target_pairs={{0,32},{32,0},{64,96},{96,64},{128,160},{160,128},{192,224},{224,1... | collective-permute-start | bytes 884744 | tf_op jit(solution)/shard_map/ppermute | solution.py:341
  52.3 12.7 %collective-permute-start.8 = (bf16[192,768]{1,0:T(8,128)(2,1)S(1)}, bf16[192,768]{1,0:T(8,128)(2,1)S(1)}, u32[]{:S(2)}, u32[]{:S(2)}) collective-permute-start(bf16[192,768]{1,0:T(8,128)(2,1)S(1)} %get-tuple-element.38.block_ref), channel_id=1, source_target_pairs={{0,64},{32,96},{64,128},{96,160},{128,192},{160,224},{192,0},{224,... | collective-permute-start | bytes 884744 | tf_op jit(solution)/shard_map/ppermute | solution.py:341
  52.5 16.3 %collective-permute-start.9 = (bf16[192,768]{1,0:T(8,128)(2,1)S(1)}, bf16[192,768]{1,0:T(8,128)(2,1)S(1)}, u32[]{:S(2)}, u32[]{:S(2)}) collective-permute-start(bf16[192,768]{1,0:T(8,128)(2,1)S(1)} %get-tuple-element.38.block_ref), channel_id=1, source_target_pairs={{0,192},{32,224},{64,0},{96,32},{128,64},{160,96},{192,128},{224,1... | collective-permute-start | bytes 884744 | tf_op jit(solution)/shard_map/ppermute | solution.py:341
  55.0 8.9 %collective-permute-start.3 = (bf16[96,768]{1,0:T(8,128)(2,1)S(1)}, bf16[96,768]{1,0:T(8,128)(2,1)S(1)}, u32[]{:S(2)}, u32[]{:S(2)}) collective-permute-start(bf16[96,768]{1,0:T(8,128)(2,1)S(1)} %get-tuple-element.49), channel_id=1, source_target_pairs={{0,128},{32,160},{64,192},{96,224},{128,0},{160,32},{192,64},{224,... | collective-permute-start | bytes 442376 | tf_op jit(solution)/shard_map/ppermute | solution.py:341
  60.1 11.3 %collective-permute-start.6 = (bf16[192,768]{1,0:T(8,128)(2,1)S(1)}, bf16[192,768]{1,0:T(8,128)(2,1)S(1)}, u32[]{:S(2)}, u32[]{:S(2)}) collective-permute-start(bf16[192,768]{1,0:T(8,128)(2,1)S(1)} %collective-permute-done.5.refs_2_), channel_id=1, source_target_pairs={{0,64},{32,96},{64,128},{96,160},{128,192},{160,224},{192,0},{224,... | collective-permute-start | bytes 884744 | tf_op jit(solution)/shard_map/ppermute | solution.py:341
  60.4 11.0 %collective-permute-start.7 = (bf16[192,768]{1,0:T(8,128)(2,1)S(1)}, bf16[192,768]{1,0:T(8,128)(2,1)S(1)}, u32[]{:S(2)}, u32[]{:S(2)}) collective-permute-start(bf16[192,768]{1,0:T(8,128)(2,1)S(1)} %collective-permute-done.5.refs_2_), channel_id=1, source_target_pairs={{0,192},{32,224},{64,0},{96,32},{128,64},{160,96},{192,128},{224,1... | collective-permute-start | bytes 884744 | tf_op jit(solution)/shard_map/ppermute | solution.py:341
  63.9 6.1 %collective-permute-start.2 = (bf16[96,768]{1,0:T(8,128)(2,1)S(1)}, bf16[96,768]{1,0:T(8,128)(2,1)S(1)}, u32[]{:S(2)}, u32[]{:S(2)}) collective-permute-start(bf16[96,768]{1,0:T(8,128)(2,1)S(1)} %shard_map.141.refs_0_), channel_id=1, source_target_pairs={{0,32},{32,0},{64,96},{96,64},{128,160},{160,128},{192,224},{224,1... | collective-permute-start | bytes 442376 | tf_op jit(solution)/shard_map/ppermute | solution.py:341
  65.0 4.9 %collective-permute-start.4 = (bf16[96,768]{1,0:T(8,128)(2,1)S(1)}, bf16[96,768]{1,0:T(8,128)(2,1)S(1)}, u32[]{:S(2)}, u32[]{:S(2)}) collective-permute-start(bf16[96,768]{1,0:T(8,128)(2,1)S(1)} %collective-permute-done.3.refs_1_), channel_id=1, source_target_pairs={{0,32},{32,0},{64,96},{96,64},{128,160},{160,128},{192,224},{224,1... | collective-permute-start | bytes 442376 | tf_op jit(solution)/shard_map/ppermute | solution.py:341
  65.3 1.7 %copy-start.3 = (f32[768,768]{1,0:T(8,128)S(1)}, f32[768,768]{1,0:T(8,128)}, u32[]{:S(2)}) copy-start(f32[768,768]{1,0:T(8,128)} %copy-done.2) | copy-start | bytes 7077892
where the time goes:
time: 73.2 us; the launch traced here: 72.4 us
  blocking collectives  21.2 us (29%)
  starting transfers between devices  21 us (29%)
  waiting for transfers between devices  16.1 us (22%)
  Pallas kernels  8.22 us (11%)
  local copies, waits for them, and re-layouts  5.06 us (7%)
  between operations  0.77 us (1%)
    all_to_all x2, blocking collectives, everyone(): return lax.all_to_all(value, axes, 0, 0, tiled=True)  21.2 us
    all_to_all x1, starting transfers between devices, everyone(): return lax.all_to_all(value, axes, 0, 0, tiled=True)  10.6 us
    ppermute x9, starting transfers between devices, moved(): return lax.ppermute(value, ROW, pairs)  8.35 us
    pallas_call x9, Pallas kernels, call(): pl.pallas_call(kernel, out_shape=outs, in_specs=in_specs or [ON_CHIP] * l...  8.22 us
    all_to_all x1, waiting for transfers between devices, everyone(): return lax.all_to_all(value, axes, 0, 0, tiled=True)  7.86 us
    ppermute x9, waiting for transfers between devices, moved(): return lax.ppermute(value, ROW, pairs)  7.44 us
    unnamed x20, local copies, waits for them, and re-layouts  5.06 us
    ppermute x1, starting transfers between devices, other_core(): return lax.ppermute(value, CORE, [(0, 1), (1, 0)])  2.06 us
  transfers between devices with their start and end apart: 11, of which 5 were waited for; matrix products, arithmetic and copies ran while one was open for 0% of the time, Pallas kernels for 5%

commit v1 on v0

--- a/solution.py
+++ b/solution.py
@@ -85,7 +85,7 @@
     ]
     ga_copy = pltpu.make_async_copy(ga_hbm, ga_ref, sems.at[2 * blocks])
     pa_copy = pltpu.make_async_copy(pa_hbm, pa_ref, sems.at[2 * blocks + 1])
-    for copy in (*g_copies, ga_copy, *p_copies, pa_copy):
+    for copy in (ga_copy, *g_copies, *p_copies, pa_copy):
         copy.start()
     lane_ref[pl.ds(rows, 2 * LANES), :] = jnp.zeros((2 * LANES, LANES), F32)
 
@@ -106,15 +106,15 @@
         return step
 
     eight = jnp.zeros((8, cols), F32)
+    ga_copy.wait()
+    row_sum = lax.fori_loop(0, attn_cols // SLAB, squares(ga_ref, 0, rows), jnp.zeros((8, rows), F32), unroll=4)
+    rows_ref[:, pl.ds(rows, rows)] = jnp.sum(row_sum, axis=0, keepdims=True)
     steps = LANES // SLAB
     col_sum = eight
     for b, copy in enumerate(g_copies):
         copy.wait()
         col_sum = lax.fori_loop(0, steps, squares(g_ref, b * LANES, 0), col_sum, unroll=True)
         rows_ref[:, pl.ds(b * LANES, LANES)] = turned_sum(lane_ref, b * LANES)
-    ga_copy.wait()
-    row_sum = lax.fori_loop(0, attn_cols // SLAB, squares(ga_ref, 0, rows), jnp.zeros((8, rows), F32), unroll=4)
-    rows_ref[:, pl.ds(rows, rows)] = jnp.sum(row_sum, axis=0, keepdims=True)
     rows_ref[...] += jnp.concatenate(
         [jnp.full((1, rows), cols * TINY_SQUARE, F32), jnp.full((1, rows), attn_cols * TINY_SQUARE, F32)], axis=1
     )
@@ -237,9 +237,9 @@
     return p - g * wide(scale, g.shape[1]) * along
 
 
-def attn_kernel(count, got_ref, attn_cols_ref, ga_ref, pa_ref, attn_ref, block_ref, rest_ref):
+def attn_kernel(count, got_ref, attn_cols_ref, ga_ref, pa_ref, attn_ref, block_ref, *part_refs):
     attn_cols, rows = ga_ref.shape
-    early = attn_cols - rest_ref.shape[0]
+    part = attn_cols // len(part_refs)
     across = attn_scales(count, got_ref, attn_cols_ref)
     along = jnp.broadcast_to(lax.rsqrt(new_rows(got_ref, 1, rows // 2)), (SLAB, rows))
     for at in range(0, attn_cols, SLAB):
@@ -247,8 +247,7 @@
         value = attn_new(ga_ref[rows_at, :].astype(F32), pa_ref[rows_at, :], at, across, along)
         attn_ref[pl.ds(at, SLAB), :] = value
         block_ref[pl.ds(at, SLAB), :] = value.astype(BF16)
-        if at >= early:
-            rest_ref[pl.ds(at - early, SLAB), :] = value.astype(BF16)
+        part_refs[at // part][pl.ds(at % part, SLAB), :] = value.astype(BF16)
 
 
 def early_kernel(count, got_ref, attn_cols_ref, ahead_ref, out_ref):
@@ -365,7 +364,6 @@
     counts = (rows_total * widths[0], rows_total * widths[1])
     attn_grad, attn_param = attn_grad.T, attn_param.T
     blocks = rows // LANES
-    early = attn_cols // 2 // SLAB * SLAB
 
     sent, row_sums, p_sums, g, ga, p, pa = call(
         sums_kernel,
@@ -384,7 +382,7 @@
             pltpu.VMEM((rows + 2 * LANES, LANES), F32),
             pltpu.SemaphoreType.DMA((2 * blocks + 2,)),
         ],
-        limit=119 << 19,
+        limit=118 << 19,
     )
     got = everyone(sent, ROW)
     cols_new, attn_cols_new, kept, sent, ahead = call(
@@ -394,7 +392,7 @@
             pltpu.VMEM((attn_cols,), F32),
             pltpu.VMEM((1, 4 * half), F32),
             pltpu.VMEM((1, 4 * half), F32),
-            pltpu.VMEM((3 * early, rows), BF16),
+            pltpu.VMEM((3 * attn_cols, rows), BF16),
         ],
         (got, row_sums, g, ga, pa, mlp_col_state, attn_col_state),
         scratch=[pltpu.VMEM((rows, LANES), F32)],
@@ -413,27 +411,29 @@
     )
     got = everyone(sent, (*ROW, CORE))
     ahead = moved(ahead, 2, 0)
-    attn_new, block, rest = call(
+    attn_new, block, *parts = call(
         functools.partial(attn_kernel, counts[1]),
         [
             pltpu.VMEM((attn_cols, rows), F32),
             pltpu.VMEM((attn_cols, rows), BF16),
-            pltpu.VMEM((attn_cols - early, rows), BF16),
+            *[pltpu.VMEM((attn_cols // 2, rows), BF16)] * 2,
         ],
         (got, attn_cols_new, ga, pa),
     )
-    (first_across,) = call(
+    (across,) = call(
         functools.partial(early_kernel, counts[1]),
-        [pltpu.VMEM((early, rows), BF16)],
+        [pltpu.VMEM((attn_cols, rows), BF16)],
         (got, attn_cols_new, ahead),
     )
-    across = moved(rest, 2, 0)
-    partner = moved(block, 0, 1)
-    left, right = moved(block, 1, 0), moved(block, 3, 0)
-    partner_first = moved(first_across, 0, 1)
+    partner = moved(parts[0], 0, 1)
+    partner_last = moved(parts[1], 0, 1)
+    left = moved(block, 1, 0)
+    right = moved(block, 3, 0)
     partner_across = moved(across, 0, 1)
     partner_left = moved(partner, 1, 0)
     partner_right = moved(partner, 3, 0)
+    last_left = moved(partner_last, 1, 0)
+    last_right = moved(partner_last, 3, 0)
     copy, attn_new, mlp_new, rows_new, cols_new, attn_rows_new, attn_cols_new = call(
         functools.partial(finish_kernel, counts[0]),
         [
@@ -457,13 +457,13 @@
     )
     copy = fill(
         copy,
-        ((2, 0, 0), (2, 0, early), (0, 1, 0), (3, 0, 0), (1, 0, 0)),
-        (first_across, across, partner, left, right),
+        ((2, 0, 0), (0, 1, 0), (0, 1, attn_cols // 2), (3, 0, 0), (1, 0, 0)),
+        (across, partner, partner_last, left, right),
     )
     copy = fill(
         copy,
-        ((2, 1, 0), (2, 1, early), (3, 1, 0), (1, 1, 0)),
-        (partner_first, partner_across, partner_left, partner_right),
+        ((2, 1, 0), (3, 1, 0), (1, 1, 0), (3, 1, attn_cols // 2), (1, 1, attn_cols // 2)),
+        (partner_across, partner_left, partner_right, last_left, last_right),
     )
     return mlp_new, attn_new.T, rows_new, cols_new, attn_rows_new, attn_cols_new, copy.T
 

time: 73.2 us -> 71 us (0.970)
  the two profiles are of different devices: /device:TPU:1 before, /device:TPU:6 now
where the time goes in v1:
time: 71 us; the launch traced here: 70.8 us
  blocking collectives  39.4 us (55%)
  starting transfers between devices  12.4 us (17%)
  waiting for transfers between devices  10.6 us (15%)
  Pallas kernels  7.63 us (11%)
  between operations  0.74 us (1%)
    all_to_all x3, blocking collectives, everyone(): return lax.all_to_all(value, axes, 0, 0, tiled=True)  39.4 us
    ppermute x10, starting transfers between devices, moved(): return lax.ppermute(value, ROW, pairs)  12.4 us
    ppermute x10, waiting for transfers between devices, moved(): return lax.ppermute(value, ROW, pairs)  9.4 us
    pallas_call x9, Pallas kernels, call(): pl.pallas_call(kernel, out_shape=outs, in_specs=in_specs or [ON_CHIP] * l...  7.63 us
  transfers between devices with their start and end apart: 11, of which 5 were waited for; matrix products, arithmetic and copies ran while one was open for 0% of the time, Pallas kernels for 5%

profile of v1, /device:TPU:6, one launch (start us, length us, event | category | flops | bytes accessed | tf_op | source)
XLA Modules:
  0.0 70.8 jit_solution(13198848887847048578)
XLA Ops:
  0.7 2.5 %shard_map.135 = (f32[8,1,1024]{2,1,0:T(1,128)S(1)}, f32[1,1536]{1,0:T(1,128)S(1)}, f32[1,256]{1,0:T(1,128)S(1)}, bf16[768,768]{1,0:T(8,128)(2,1)S(1)}, bf16[192...) custom-call(bf16[768,768]{1,0:T(8,128)(2,1)} %g_hbm.1, bf16[192,768]{1,0:T(8,128)(2,1)} %bitcast.6, ...), custom_call_target="tpu_custom_call" | custom-call | tf_op jit(solution)/shard_map/pallas_call | solution.py:30
  3.1 0.0 copy-start.1
  3.2 0.0 copy-start.2
  3.2 9.7 %all_to_all.15.got_ref = f32[8,1,1024]{2,1,0:T(1,128)S(1)} all-to-all(f32[8,1,1024]{2,1,0:T(1,128)S(1)} %get-tuple-element.30), channel_id=1, replica_groups=mesh['row_0'=4,'row_1'=2,'col_0'=2,'col_1'=8,'col_2'=2] {'row_0','row_1'}, dimensions={0} | all-to-all | bytes 65536 | tf_op jit(solution)/shard_map/all_to_all | solution.py:334
  12.9 0.7 %shard_map.136 = (f32[768]{0:T(1024)S(1)}, f32[192]{0:T(256)S(1)}, f32[1,1536]{1,0:T(1,128)S(1)}, f32[1,1536]{1,0:T(1,128)S(1)}, bf16[576,768]{1,0:T(8,128)(2,1)S(1)}) custom-call(f32[8,1,1024]{2,1,0:T(1,128)S(1)} %all_to_all.15.got_ref, f32[1,1536]{1,0:T(1,128)S(1)} %get-tuple-element.31.rows_ref, bf16[768,768]{1,0:T(8,128)(2,1)S(1)} %get-tuple-element.32.g_ref, ...), custom_call_target="tpu_custom_call" | custom-call | tf_op jit(solution)/shard_map/pallas_call | solution.py:30
  13.6 2.2 %collective-permute-start.1 = (bf16[576,768]{1,0:T(8,128)(2,1)S(1)}, bf16[576,768]{1,0:T(8,128)(2,1)S(1)}, u32[]{:S(2)}, u32[]{:S(2)}) collective-permute-start(bf16[576,768]{1,0:T(8,128)(2,1)S(1)} %get-tuple-element.49), channel_id=1, source_target_pairs={{0,128},{32,160},{64,192},{96,224},{128,0},{160,32},{192,64},{224,... | collective-permute-start | bytes 2654216 | tf_op jit(solution)/shard_map/ppermute | solution.py:340
  15.8 0.0 collective-permute-start
  15.8 1.2 %collective-permute-done.got_ref = f32[1,1536]{1,0:T(1,128)S(1)} collective-permute-done((f32[1,1536]{1,0:T(1,128)S(1)}, f32[1,1536]{1,0:T(1,128)S(1)}, u32[]{:S(2)}, u32[]{:S(2)}) %collective-permute-start) | collective-permute-done | bytes 6176 | tf_op jit(solution)/shard_map/ppermute | solution.py:344
  17.0 20.9 %all_to_all.16.got_ref = f32[16,1,1792]{2,1,0:T(1,128)S(1)} all-to-all(f32[16,1,1792]{2,1,0:T(1,128)S(1)} %shard_map.137), channel_id=1, replica_groups=mesh['row_0'=4,'row_1'=2,'col_0'=2,'col_1'=8,'col_2'=2] {'col_0','col_1'}, dimensions={0} | all-to-all | bytes 229376 | tf_op jit(solution)/shard_map/all_to_all | solution.py:334
  38.0 8.8 %all_to_all.17.got_ref = f32[16,1,1280]{2,1,0:T(1,128)S(1)} all-to-all(f32[16,1,1280]{2,1,0:T(1,128)S(1)} %shard_map.138), channel_id=1, replica_groups=mesh['row_0'=4,'row_1'=2,'col_0'=2,'col_1'=8,'col_2'=2] {'row_0','row_1'..., dimensions={0} | all-to-all | bytes 163840 | tf_op jit(solution)/shard_map/all_to_all | solution.py:334
  46.7 0.3 shard_map.139
  47.0 0.8 %collective-permute-start.10 = (bf16[192,768]{1,0:T(8,128)(2,1)S(1)}, bf16[192,768]{1,0:T(8,128)(2,1)S(1)}, u32[]{:S(2)}, u32[]{:S(2)}) collective-permute-start(bf16[192,768]{1,0:T(8,128)(2,1)S(1)} %get-tuple-element.39.block_ref), channel_id=1, source_target_pairs={{0,192},{32,224},{64,0},{96,32},{128,64},{160,96},{192,128},{224,1... | collective-permute-start | bytes 884744 | tf_op jit(solution)/shard_map/ppermute | solution.py:340
  47.8 2.6 %collective-permute-start.9 = (bf16[192,768]{1,0:T(8,128)(2,1)S(1)}, bf16[192,768]{1,0:T(8,128)(2,1)S(1)}, u32[]{:S(2)}, u32[]{:S(2)}) collective-permute-start(bf16[192,768]{1,0:T(8,128)(2,1)S(1)} %get-tuple-element.39.block_ref), channel_id=1, source_target_pairs={{0,64},{32,96},{64,128},{96,160},{128,192},{160,224},{192,0},{224,... | collective-permute-start | bytes 884744 | tf_op jit(solution)/shard_map/ppermute | solution.py:340
  50.3 0.6 collective-permute-start.3
  50.9 1.4 %collective-permute-start.6 = (bf16[96,768]{1,0:T(8,128)(2,1)S(1)}, bf16[96,768]{1,0:T(8,128)(2,1)S(1)}, u32[]{:S(2)}, u32[]{:S(2)}) collective-permute-start(bf16[96,768]{1,0:T(8,128)(2,1)S(1)} %get-tuple-element.51), channel_id=1, source_target_pairs={{0,32},{32,0},{64,96},{96,64},{128,160},{160,128},{192,224},{224,1... | collective-permute-start | bytes 442376 | tf_op jit(solution)/shard_map/ppermute | solution.py:340
  52.4 0.0 collective-permute-done.1.ahead_ref
  52.4 0.3 shard_map.141.refs_0_
  52.6 0.7 collective-permute-start.2
  53.3 3.7 %collective-permute-done.3.refs_1_ = bf16[96,768]{1,0:T(8,128)(2,1)S(1)} collective-permute-done((bf16[96,768]{1,0:T(8,128)(2,1)S(1)}, bf16[96,768]{1,0:T(8,128)(2,1)S(1)}, u32[]{:S(2)}, u32[]{:S(2)}) %collective-permute-start.3) | collective-permute-done | bytes 147488 | tf_op jit(solution)/shard_map/ppermute | solution.py:340
  57.0 0.9 %collective-permute-start.4 = (bf16[96,768]{1,0:T(8,128)(2,1)S(1)}, bf16[96,768]{1,0:T(8,128)(2,1)S(1)}, u32[]{:S(2)}, u32[]{:S(2)}) collective-permute-start(bf16[96,768]{1,0:T(8,128)(2,1)S(1)} %collective-permute-done.3.refs_1_), channel_id=1, source_target_pairs={{0,64},{32,96},{64,128},{96,160},{128,192},{160,224},{192,0},{224,... | collective-permute-start | bytes 442376 | tf_op jit(solution)/shard_map/ppermute | solution.py:340
  58.0 2.2 %collective-permute-done.6.refs_2_ = bf16[96,768]{1,0:T(8,128)(2,1)S(1)} collective-permute-done((bf16[96,768]{1,0:T(8,128)(2,1)S(1)}, bf16[96,768]{1,0:T(8,128)(2,1)S(1)}, u32[]{:S(2)}, u32[]{:S(2)}) %collective-permute-start.6) | collective-permute-done | bytes 147488 | tf_op jit(solution)/shard_map/ppermute | solution.py:340
  60.2 3.2 %collective-permute-start.7 = (bf16[96,768]{1,0:T(8,128)(2,1)S(1)}, bf16[96,768]{1,0:T(8,128)(2,1)S(1)}, u32[]{:S(2)}, u32[]{:S(2)}) collective-permute-start(bf16[96,768]{1,0:T(8,128)(2,1)S(1)} %collective-permute-done.6.refs_2_), channel_id=1, source_target_pairs={{0,64},{32,96},{64,128},{96,160},{128,192},{160,224},{192,0},{224,... | collective-permute-start | bytes 442376 | tf_op jit(solution)/shard_map/ppermute | solution.py:340
  63.4 0.0 collective-permute-done.9.refs_3_
  63.4 0.0 collective-permute-start.8
  63.5 1.8 %shard_map.140 = (bf16[192,6144]{1,0:T(8,128)(2,1)}, f32[192,768]{1,0:T(8,128)}, f32[768,768]{1,0:T(8,128)}, f32[768]{0:T(1024)}, f32[768]{0:T(1024)}, /*index=5*/f32[768]{0:T(1024)}, f32[192]{0:T(256)}) custom-call(bf16[192,768]{1,0:T(8,128)(2,1)S(1)} %get-tuple-element.39.block_ref, f32[16,1,1280]{2,1,0:T(1,128)S(1)} %all_to_all.17.got_ref, ...), custom_call_target="tpu_custom_call" | custom-call | flops 4194304 | bytes 4194304 | tf_op jit(solution)/shard_map/pallas_call | solution.py:30
  65.3 1.1 %shard_map.142.refs_5_ = bf16[192,6144]{1,0:T(8,128)(2,1)} custom-call(bf16[192,768]{1,0:T(8,128)(2,1)S(1)} %shard_map.141.refs_0_, bf16[96,768]{1,0:T(8,128)(2,1)S(1)} %collective-permute-done.3.refs_1_, bf16[96,768]{1,0:T(8,128)(2,1)S(1)} %collective-permute-done.6.refs_2_, ...), custom_call_target="tpu_custom_call", output_to_operand_aliasing={{}: (5, {})} | custom-call | tf_op jit(solution)/shard_map/pallas_call | solution.py:30
  66.4 0.0 collective-permute-done.4.refs_1_
  66.4 0.8 %collective-permute-done.5.refs_2_ = bf16[96,768]{1,0:T(8,128)(2,1)S(1)} collective-permute-done((bf16[96,768]{1,0:T(8,128)(2,1)S(1)}, bf16[96,768]{1,0:T(8,128)(2,1)S(1)}, u32[]{:S(2)}, u32[]{:S(2)}) %collective-permute-start.5) | collective-permute-done | bytes 147488 | tf_op jit(solution)/shard_map/ppermute | solution.py:340
  67.1 0.0 collective-permute-done.7.refs_3_
  67.1 2.7 %collective-permute-done.8.refs_4_ = bf16[96,768]{1,0:T(8,128)(2,1)S(1)} collective-permute-done((bf16[96,768]{1,0:T(8,128)(2,1)S(1)}, bf16[96,768]{1,0:T(8,128)(2,1)S(1)}, u32[]{:S(2)}, u32[]{:S(2)}) %collective-permute-start.8) | collective-permute-done | bytes 147488 | tf_op jit(solution)/shard_map/ppermute | solution.py:340
  69.8 0.0 collective-permute-done.2.refs_0_
  69.8 0.9 %shard_map.143 = bf16[192,6144]{1,0:T(8,128)(2,1)} custom-call(bf16[192,768]{1,0:T(8,128)(2,1)S(1)} %collective-permute-done.2.refs_0_, bf16[96,768]{1,0:T(8,128)(2,1)S(1)} %collective-permute-done.4.refs_1_, bf16[96,768]{1,0:T(8,128)(2,1)S(1)} %collective-permute-done.5.refs_2_, ...), custom_call_target="tpu_custom_call", output_to_operand_aliasing={{}: (5, {})} | custom-call | tf_op jit(solution)/shard_map/pallas_call | solution.py:30
  (10 shorter events, 0.1 us)
Async XLA Ops:
  0.6 12.3 %copy-start = (f32[768]{0:T(1024)S(1)}, f32[768]{0:T(1024)}, u32[]{:S(2)}) copy-start(f32[768]{0:T(1024)} %state_ref.2) | copy-start | bytes 9220
  0.6 12.3 %copy-start.3 = (f32[192]{0:T(256)S(1)}, f32[192]{0:T(256)}, u32[]{:S(2)}) copy-start(f32[192]{0:T(256)} %attn_state_ref.2) | copy-start | bytes 2308
  3.1 34.8 %copy-start.1 = (f32[768]{0:T(1024)S(1)}, f32[768]{0:T(1024)}, u32[]{:S(2)}) copy-start(f32[768]{0:T(1024)} %state_ref.3) | copy-start | bytes 9220
  3.2 34.8 %copy-start.2 = (f32[768]{0:T(1024)S(1)}, f32[768]{0:T(1024)}, u32[]{:S(2)}) copy-start(f32[768]{0:T(1024)} %attn_state_ref.3) | copy-start | bytes 9220
  13.6 38.7 %collective-permute-start.1 = (bf16[576,768]{1,0:T(8,128)(2,1)S(1)}, bf16[576,768]{1,0:T(8,128)(2,1)S(1)}, u32[]{:S(2)}, u32[]{:S(2)}) collective-permute-start(bf16[576,768]{1,0:T(8,128)(2,1)S(1)} %get-tuple-element.49), channel_id=1, source_target_pairs={{0,128},{32,160},{64,192},{96,224},{128,0},{160,32},{192,64},{224,... | collective-permute-start | bytes 2654216 | tf_op jit(solution)/shard_map/ppermute | solution.py:340
  15.8 1.2 %collective-permute-start = (f32[1,1536]{1,0:T(1,128)S(1)}, f32[1,1536]{1,0:T(1,128)S(1)}, u32[]{:S(2)}, u32[]{:S(2)}) collective-permute-start(f32[1,1536]{1,0:T(1,128)S(1)} %get-tuple-element.36), channel_id=1, source_target_pairs={{0,1},{1,0},{2,3},{3,2},{4,5},{5,4},{6,7},{7,6},{8,9},{9,8},{10,11... | collective-permute-start | bytes 18440 | tf_op jit(solution)/shard_map/ppermute | solution.py:344
  47.0 13.2 %collective-permute-start.10 = (bf16[192,768]{1,0:T(8,128)(2,1)S(1)}, bf16[192,768]{1,0:T(8,128)(2,1)S(1)}, u32[]{:S(2)}, u32[]{:S(2)}) collective-permute-start(bf16[192,768]{1,0:T(8,128)(2,1)S(1)} %get-tuple-element.39.block_ref), channel_id=1, source_target_pairs={{0,192},{32,224},{64,0},{96,32},{128,64},{160,96},{192,128},{224,1... | collective-permute-start | bytes 884744 | tf_op jit(solution)/shard_map/ppermute | solution.py:340
  47.8 15.7 %collective-permute-start.9 = (bf16[192,768]{1,0:T(8,128)(2,1)S(1)}, bf16[192,768]{1,0:T(8,128)(2,1)S(1)}, u32[]{:S(2)}, u32[]{:S(2)}) collective-permute-start(bf16[192,768]{1,0:T(8,128)(2,1)S(1)} %get-tuple-element.39.block_ref), channel_id=1, source_target_pairs={{0,64},{32,96},{64,128},{96,160},{128,192},{160,224},{192,0},{224,... | collective-permute-start | bytes 884744 | tf_op jit(solution)/shard_map/ppermute | solution.py:340
  50.3 6.7 %collective-permute-start.3 = (bf16[96,768]{1,0:T(8,128)(2,1)S(1)}, bf16[96,768]{1,0:T(8,128)(2,1)S(1)}, u32[]{:S(2)}, u32[]{:S(2)}) collective-permute-start(bf16[96,768]{1,0:T(8,128)(2,1)S(1)} %get-tuple-element.50), channel_id=1, source_target_pairs={{0,32},{32,0},{64,96},{96,64},{128,160},{160,128},{192,224},{224,1... | collective-permute-start | bytes 442376 | tf_op jit(solution)/shard_map/ppermute | solution.py:340
  50.9 9.3 %collective-permute-start.6 = (bf16[96,768]{1,0:T(8,128)(2,1)S(1)}, bf16[96,768]{1,0:T(8,128)(2,1)S(1)}, u32[]{:S(2)}, u32[]{:S(2)}) collective-permute-start(bf16[96,768]{1,0:T(8,128)(2,1)S(1)} %get-tuple-element.51), channel_id=1, source_target_pairs={{0,32},{32,0},{64,96},{96,64},{128,160},{160,128},{192,224},{224,1... | collective-permute-start | bytes 442376 | tf_op jit(solution)/shard_map/ppermute | solution.py:340
  52.6 17.2 %collective-permute-start.2 = (bf16[192,768]{1,0:T(8,128)(2,1)S(1)}, bf16[192,768]{1,0:T(8,128)(2,1)S(1)}, u32[]{:S(2)}, u32[]{:S(2)}) collective-permute-start(bf16[192,768]{1,0:T(8,128)(2,1)S(1)} %shard_map.141.refs_0_), channel_id=1, source_target_pairs={{0,32},{32,0},{64,96},{96,64},{128,160},{160,128},{192,224},{224,1... | collective-permute-start | bytes 884744 | tf_op jit(solution)/shard_map/ppermute | solution.py:340
  57.0 9.3 %collective-permute-start.4 = (bf16[96,768]{1,0:T(8,128)(2,1)S(1)}, bf16[96,768]{1,0:T(8,128)(2,1)S(1)}, u32[]{:S(2)}, u32[]{:S(2)}) collective-permute-start(bf16[96,768]{1,0:T(8,128)(2,1)S(1)} %collective-permute-done.3.refs_1_), channel_id=1, source_target_pairs={{0,64},{32,96},{64,128},{96,160},{128,192},{160,224},{192,0},{224,... | collective-permute-start | bytes 442376 | tf_op jit(solution)/shard_map/ppermute | solution.py:340
  60.2 6.9 %collective-permute-start.5 = (bf16[96,768]{1,0:T(8,128)(2,1)S(1)}, bf16[96,768]{1,0:T(8,128)(2,1)S(1)}, u32[]{:S(2)}, u32[]{:S(2)}) collective-permute-start(bf16[96,768]{1,0:T(8,128)(2,1)S(1)} %collective-permute-done.3.refs_1_), channel_id=1, source_target_pairs={{0,192},{32,224},{64,0},{96,32},{128,64},{160,96},{192,128},{224,1... | collective-permute-start | bytes 442376 | tf_op jit(solution)/shard_map/ppermute | solution.py:340
  60.2 6.9 %collective-permute-start.7 = (bf16[96,768]{1,0:T(8,128)(2,1)S(1)}, bf16[96,768]{1,0:T(8,128)(2,1)S(1)}, u32[]{:S(2)}, u32[]{:S(2)}) collective-permute-start(bf16[96,768]{1,0:T(8,128)(2,1)S(1)} %collective-permute-done.6.refs_2_), channel_id=1, source_target_pairs={{0,64},{32,96},{64,128},{96,160},{128,192},{160,224},{192,0},{224,... | collective-permute-start | bytes 442376 | tf_op jit(solution)/shard_map/ppermute | solution.py:340
  63.4 6.4 %collective-permute-start.8 = (bf16[96,768]{1,0:T(8,128)(2,1)S(1)}, bf16[96,768]{1,0:T(8,128)(2,1)S(1)}, u32[]{:S(2)}, u32[]{:S(2)}) collective-permute-start(bf16[96,768]{1,0:T(8,128)(2,1)S(1)} %collective-permute-done.6.refs_2_), channel_id=1, source_target_pairs={{0,192},{32,224},{64,0},{96,32},{128,64},{160,96},{192,128},{224,1... | collective-permute-start | bytes 442376 | tf_op jit(solution)/shard_map/ppermute | solution.py:340

commit v2 on v1

--- a/solution.py
+++ b/solution.py
@@ -259,8 +259,16 @@
         out_ref[pl.ds(at, SLAB), :] = attn_new(g, high + low, at, across, along).astype(BF16)
 
 
+NEAR, FAR = "near", "far"
+
+
 def place(dx, dy):
-    x = lax.rem(lax.axis_index("row_0") + dx, lax.axis_size("row_0"))
+    x = lax.axis_index("row_0")
+    if dx == NEAR:
+        dx = 1 + 2 * lax.rem(x, 2)
+    elif dx == FAR:
+        dx = 3 - 2 * lax.rem(x, 2)
+    x = lax.rem(x + dx, lax.axis_size("row_0"))
     y = lax.rem(lax.axis_index("row_1") + dy, lax.axis_size("row_1"))
     return x * lax.axis_size("row_1") + y
 
@@ -336,7 +344,8 @@
 
 def moved(value, dx, dy):
     xs, ys = lax.axis_size("row_0"), lax.axis_size("row_1")
-    pairs = [(x * ys + y, (x + dx) % xs * ys + (y + dy) % ys) for x in range(xs) for y in range(ys)]
+    steps = {NEAR: (1, xs - 1), FAR: (xs - 1, 1)}.get(dx, (dx, dx))
+    pairs = [(x * ys + y, (x + steps[x % 2]) % xs * ys + (y + dy) % ys) for x in range(xs) for y in range(ys)]
     return lax.ppermute(value, ROW, pairs)
 
 
@@ -427,13 +436,13 @@
     )
     partner = moved(parts[0], 0, 1)
     partner_last = moved(parts[1], 0, 1)
-    left = moved(block, 1, 0)
-    right = moved(block, 3, 0)
+    near = moved(block, NEAR, 0)
+    far = moved(block, FAR, 0)
     partner_across = moved(across, 0, 1)
-    partner_left = moved(partner, 1, 0)
-    partner_right = moved(partner, 3, 0)
-    last_left = moved(partner_last, 1, 0)
-    last_right = moved(partner_last, 3, 0)
+    partner_near = moved(partner, NEAR, 0)
+    partner_far = moved(partner, FAR, 0)
+    last_near = moved(partner_last, NEAR, 0)
+    last_far = moved(partner_last, FAR, 0)
     copy, attn_new, mlp_new, rows_new, cols_new, attn_rows_new, attn_cols_new = call(
         functools.partial(finish_kernel, counts[0]),
         [
@@ -457,13 +466,13 @@
     )
     copy = fill(
         copy,
-        ((2, 0, 0), (0, 1, 0), (0, 1, attn_cols // 2), (3, 0, 0), (1, 0, 0)),
-        (across, partner, partner_last, left, right),
+        ((2, 0, 0), (0, 1, 0), (0, 1, attn_cols // 2), (NEAR, 0, 0), (FAR, 0, 0)),
+        (across, partner, partner_last, near, far),
     )
     copy = fill(
         copy,
-        ((2, 1, 0), (3, 1, 0), (1, 1, 0), (3, 1, attn_cols // 2), (1, 1, attn_cols // 2)),
-        (partner_across, partner_left, partner_right, last_left, last_right),
+        ((2, 1, 0), (NEAR, 1, 0), (FAR, 1, 0), (NEAR, 1, attn_cols // 2), (FAR, 1, attn_cols // 2)),
+        (partner_across, partner_near, partner_far, last_near, last_far),
     )
     return mlp_new, attn_new.T, rows_new, cols_new, attn_rows_new, attn_cols_new, copy.T
 

time: 71 us -> 70.1 us (0.987)
  the two profiles are of different devices: /device:TPU:6 before, /device:TPU:32 now
where the time goes in v2:
time: 70.1 us; the launch traced here: 69.9 us
  blocking collectives  41.2 us (59%)
  starting transfers between devices  11.9 us (17%)
  waiting for transfers between devices  8.4 us (12%)
  Pallas kernels  7.63 us (11%)
  between operations  0.75 us (1%)
    all_to_all x3, blocking collectives, everyone(): return lax.all_to_all(value, axes, 0, 0, tiled=True)  41.2 us
    ppermute x10, starting transfers between devices, moved(): return lax.ppermute(value, ROW, pairs)  11.9 us
    pallas_call x9, Pallas kernels, call(): pl.pallas_call(kernel, out_shape=outs, in_specs=in_specs or [ON_CHIP] * l...  7.63 us
    ppermute x10, waiting for transfers between devices, moved(): return lax.ppermute(value, ROW, pairs)  7.24 us
  transfers between devices with their start and end apart: 11, of which 4 were waited for; matrix products, arithmetic and copies ran while one was open for 0% of the time, Pallas kernels for 5%

profile of v2, /device:TPU:32, one launch (start us, length us, event | category | flops | bytes accessed | tf_op | source)
XLA Modules:
  0.0 69.9 jit_solution(10142073090068382372)
XLA Ops:
  0.7 2.5 %shard_map.135 = (f32[8,1,1024]{2,1,0:T(1,128)S(1)}, f32[1,1536]{1,0:T(1,128)S(1)}, f32[1,256]{1,0:T(1,128)S(1)}, bf16[768,768]{1,0:T(8,128)(2,1)S(1)}, bf16[192...) custom-call(bf16[768,768]{1,0:T(8,128)(2,1)} %g_hbm.1, bf16[192,768]{1,0:T(8,128)(2,1)} %bitcast.6, ...), custom_call_target="tpu_custom_call" | custom-call | tf_op jit(solution)/shard_map/pallas_call | solution.py:30
  3.1 0.0 copy-start.1
  3.2 0.0 copy-start.2
  3.2 11.3 %all_to_all.15.got_ref = f32[8,1,1024]{2,1,0:T(1,128)S(1)} all-to-all(f32[8,1,1024]{2,1,0:T(1,128)S(1)} %get-tuple-element.30), channel_id=1, replica_groups=mesh['row_0'=4,'row_1'=2,'col_0'=2,'col_1'=8,'col_2'=2] {'row_0','row_1'}, dimensions={0} | all-to-all | bytes 65536 | tf_op jit(solution)/shard_map/all_to_all | solution.py:342
  14.5 0.7 %shard_map.136 = (f32[768]{0:T(1024)S(1)}, f32[192]{0:T(256)S(1)}, f32[1,1536]{1,0:T(1,128)S(1)}, f32[1,1536]{1,0:T(1,128)S(1)}, bf16[576,768]{1,0:T(8,128)(2,1)S(1)}) custom-call(f32[8,1,1024]{2,1,0:T(1,128)S(1)} %all_to_all.15.got_ref, f32[1,1536]{1,0:T(1,128)S(1)} %get-tuple-element.31.rows_ref, bf16[768,768]{1,0:T(8,128)(2,1)S(1)} %get-tuple-element.32.g_ref, ...), custom_call_target="tpu_custom_call" | custom-call | tf_op jit(solution)/shard_map/pallas_call | solution.py:30
  15.2 1.3 %collective-permute-start.1 = (bf16[576,768]{1,0:T(8,128)(2,1)S(1)}, bf16[576,768]{1,0:T(8,128)(2,1)S(1)}, u32[]{:S(2)}, u32[]{:S(2)}) collective-permute-start(bf16[576,768]{1,0:T(8,128)(2,1)S(1)} %get-tuple-element.49), channel_id=1, source_target_pairs={{0,128},{32,160},{64,192},{96,224},{128,0},{160,32},{192,64},{224,... | collective-permute-start | bytes 2654216 | tf_op jit(solution)/shard_map/ppermute | solution.py:349
  16.6 0.0 collective-permute-start
  16.6 1.2 %collective-permute-done.got_ref = f32[1,1536]{1,0:T(1,128)S(1)} collective-permute-done((f32[1,1536]{1,0:T(1,128)S(1)}, f32[1,1536]{1,0:T(1,128)S(1)}, u32[]{:S(2)}, u32[]{:S(2)}) %collective-permute-start) | collective-permute-done | bytes 6176 | tf_op jit(solution)/shard_map/ppermute | solution.py:353
  17.8 20.2 %all_to_all.16.got_ref = f32[16,1,1792]{2,1,0:T(1,128)S(1)} all-to-all(f32[16,1,1792]{2,1,0:T(1,128)S(1)} %shard_map.137), channel_id=1, replica_groups=mesh['row_0'=4,'row_1'=2,'col_0'=2,'col_1'=8,'col_2'=2] {'col_0','col_1'}, dimensions={0} | all-to-all | bytes 229376 | tf_op jit(solution)/shard_map/all_to_all | solution.py:342
  38.0 9.6 %all_to_all.17.got_ref = f32[16,1,1280]{2,1,0:T(1,128)S(1)} all-to-all(f32[16,1,1280]{2,1,0:T(1,128)S(1)} %shard_map.138), channel_id=1, replica_groups=mesh['row_0'=4,'row_1'=2,'col_0'=2,'col_1'=8,'col_2'=2] {'row_0','row_1'..., dimensions={0} | all-to-all | bytes 163840 | tf_op jit(solution)/shard_map/all_to_all | solution.py:342
  47.7 0.3 shard_map.139
  48.0 1.2 %collective-permute-start.10 = (bf16[192,768]{1,0:T(8,128)(2,1)S(1)}, bf16[192,768]{1,0:T(8,128)(2,1)S(1)}, u32[]{:S(2)}, u32[]{:S(2)}) collective-permute-start(bf16[192,768]{1,0:T(8,128)(2,1)S(1)} %get-tuple-element.39.block_ref), channel_id=1, source_target_pairs={{0,192},{32,224},{64,128},{96,160},{128,64},{160,96},{192,0},{224,... | collective-permute-start | bytes 884744 | tf_op jit(solution)/shard_map/ppermute | solution.py:349
  49.1 0.1 collective-permute-start.9
  49.2 0.6 collective-permute-start.3
  49.8 1.4 %collective-permute-start.6 = (bf16[96,768]{1,0:T(8,128)(2,1)S(1)}, bf16[96,768]{1,0:T(8,128)(2,1)S(1)}, u32[]{:S(2)}, u32[]{:S(2)}) collective-permute-start(bf16[96,768]{1,0:T(8,128)(2,1)S(1)} %get-tuple-element.51), channel_id=1, source_target_pairs={{0,32},{32,0},{64,96},{96,64},{128,160},{160,128},{192,224},{224,1... | collective-permute-start | bytes 442376 | tf_op jit(solution)/shard_map/ppermute | solution.py:349
  51.3 0.3 shard_map.141.refs_0_
  51.5 0.7 %collective-permute-start.2 = (bf16[192,768]{1,0:T(8,128)(2,1)S(1)}, bf16[192,768]{1,0:T(8,128)(2,1)S(1)}, u32[]{:S(2)}, u32[]{:S(2)}) collective-permute-start(bf16[192,768]{1,0:T(8,128)(2,1)S(1)} %shard_map.141.refs_0_), channel_id=1, source_target_pairs={{0,32},{32,0},{64,96},{96,64},{128,160},{160,128},{192,224},{224,1... | collective-permute-start | bytes 884744 | tf_op jit(solution)/shard_map/ppermute | solution.py:349
  52.2 3.7 %collective-permute-done.3.refs_1_ = bf16[96,768]{1,0:T(8,128)(2,1)S(1)} collective-permute-done((bf16[96,768]{1,0:T(8,128)(2,1)S(1)}, bf16[96,768]{1,0:T(8,128)(2,1)S(1)}, u32[]{:S(2)}, u32[]{:S(2)}) %collective-permute-start.3) | collective-permute-done | bytes 147488 | tf_op jit(solution)/shard_map/ppermute | solution.py:349
  55.9 2.0 %collective-permute-start.4 = (bf16[96,768]{1,0:T(8,128)(2,1)S(1)}, bf16[96,768]{1,0:T(8,128)(2,1)S(1)}, u32[]{:S(2)}, u32[]{:S(2)}) collective-permute-start(bf16[96,768]{1,0:T(8,128)(2,1)S(1)} %collective-permute-done.3.refs_1_), channel_id=1, source_target_pairs={{0,64},{32,96},{64,0},{96,32},{128,192},{160,224},{192,128},{224,1... | collective-permute-start | bytes 442376 | tf_op jit(solution)/shard_map/ppermute | solution.py:349
  57.9 1.2 %collective-permute-done.6.refs_2_ = bf16[96,768]{1,0:T(8,128)(2,1)S(1)} collective-permute-done((bf16[96,768]{1,0:T(8,128)(2,1)S(1)}, bf16[96,768]{1,0:T(8,128)(2,1)S(1)}, u32[]{:S(2)}, u32[]{:S(2)}) %collective-permute-start.6) | collective-permute-done | bytes 147488 | tf_op jit(solution)/shard_map/ppermute | solution.py:349
  59.1 2.1 %collective-permute-start.5 = (bf16[96,768]{1,0:T(8,128)(2,1)S(1)}, bf16[96,768]{1,0:T(8,128)(2,1)S(1)}, u32[]{:S(2)}, u32[]{:S(2)}) collective-permute-start(bf16[96,768]{1,0:T(8,128)(2,1)S(1)} %collective-permute-done.3.refs_1_), channel_id=1, source_target_pairs={{0,192},{32,224},{64,128},{96,160},{128,64},{160,96},{192,0},{224,... | collective-permute-start | bytes 442376 | tf_op jit(solution)/shard_map/ppermute | solution.py:349
  61.2 0.0 collective-permute-done.10.refs_4_
  61.2 1.4 %collective-permute-start.7 = (bf16[96,768]{1,0:T(8,128)(2,1)S(1)}, bf16[96,768]{1,0:T(8,128)(2,1)S(1)}, u32[]{:S(2)}, u32[]{:S(2)}) collective-permute-start(bf16[96,768]{1,0:T(8,128)(2,1)S(1)} %collective-permute-done.6.refs_2_), channel_id=1, source_target_pairs={{0,64},{32,96},{64,0},{96,32},{128,192},{160,224},{192,128},{224,1... | collective-permute-start | bytes 442376 | tf_op jit(solution)/shard_map/ppermute | solution.py:349
  62.6 0.0 collective-permute-done.9.refs_3_
  62.6 1.1 %collective-permute-start.8 = (bf16[96,768]{1,0:T(8,128)(2,1)S(1)}, bf16[96,768]{1,0:T(8,128)(2,1)S(1)}, u32[]{:S(2)}, u32[]{:S(2)}) collective-permute-start(bf16[96,768]{1,0:T(8,128)(2,1)S(1)} %collective-permute-done.6.refs_2_), channel_id=1, source_target_pairs={{0,192},{32,224},{64,128},{96,160},{128,64},{160,96},{192,0},{224,... | collective-permute-start | bytes 442376 | tf_op jit(solution)/shard_map/ppermute | solution.py:349
  63.7 1.8 %shard_map.140 = (bf16[192,6144]{1,0:T(8,128)(2,1)}, f32[192,768]{1,0:T(8,128)}, f32[768,768]{1,0:T(8,128)}, f32[768]{0:T(1024)}, f32[768]{0:T(1024)}, /*index=5*/f32[768]{0:T(1024)}, f32[192]{0:T(256)}) custom-call(bf16[192,768]{1,0:T(8,128)(2,1)S(1)} %get-tuple-element.39.block_ref, f32[16,1,1280]{2,1,0:T(1,128)S(1)} %all_to_all.17.got_ref, ...), custom_call_target="tpu_custom_call" | custom-call | flops 4194304 | bytes 4194304 | tf_op jit(solution)/shard_map/pallas_call | solution.py:30
  65.5 1.1 %shard_map.142.refs_5_ = bf16[192,6144]{1,0:T(8,128)(2,1)} custom-call(bf16[192,768]{1,0:T(8,128)(2,1)S(1)} %shard_map.141.refs_0_, bf16[96,768]{1,0:T(8,128)(2,1)S(1)} %collective-permute-done.3.refs_1_, bf16[96,768]{1,0:T(8,128)(2,1)S(1)} %collective-permute-done.6.refs_2_, ...), custom_call_target="tpu_custom_call", output_to_operand_aliasing={{}: (5, {})} | custom-call | tf_op jit(solution)/shard_map/pallas_call | solution.py:30
  66.6 0.0 collective-permute-done.4.refs_1_
  66.6 0.0 collective-permute-done.5.refs_2_
  66.6 2.3 %collective-permute-done.8.refs_4_ = bf16[96,768]{1,0:T(8,128)(2,1)S(1)} collective-permute-done((bf16[96,768]{1,0:T(8,128)(2,1)S(1)}, bf16[96,768]{1,0:T(8,128)(2,1)S(1)}, u32[]{:S(2)}, u32[]{:S(2)}) %collective-permute-start.8) | collective-permute-done | bytes 147488 | tf_op jit(solution)/shard_map/ppermute | solution.py:349
  68.9 0.0 collective-permute-done.2.refs_0_
  68.9 0.9 %shard_map.143 = bf16[192,6144]{1,0:T(8,128)(2,1)} custom-call(bf16[192,768]{1,0:T(8,128)(2,1)S(1)} %collective-permute-done.2.refs_0_, bf16[96,768]{1,0:T(8,128)(2,1)S(1)} %collective-permute-done.4.refs_1_, bf16[96,768]{1,0:T(8,128)(2,1)S(1)} %collective-permute-done.5.refs_2_, ...), custom_call_target="tpu_custom_call", output_to_operand_aliasing={{}: (5, {})} | custom-call | tf_op jit(solution)/shard_map/pallas_call | solution.py:30
  (10 shorter events, 0.1 us)
Async XLA Ops:
  0.6 13.9 %copy-start = (f32[768]{0:T(1024)S(1)}, f32[768]{0:T(1024)}, u32[]{:S(2)}) copy-start(f32[768]{0:T(1024)} %state_ref.2) | copy-start | bytes 9220
  0.6 13.9 %copy-start.3 = (f32[192]{0:T(256)S(1)}, f32[192]{0:T(256)}, u32[]{:S(2)}) copy-start(f32[192]{0:T(256)} %attn_state_ref.2) | copy-start | bytes 2308
  3.1 34.8 %copy-start.1 = (f32[768]{0:T(1024)S(1)}, f32[768]{0:T(1024)}, u32[]{:S(2)}) copy-start(f32[768]{0:T(1024)} %state_ref.3) | copy-start | bytes 9220
  3.2 34.8 %copy-start.2 = (f32[768]{0:T(1024)S(1)}, f32[768]{0:T(1024)}, u32[]{:S(2)}) copy-start(f32[768]{0:T(1024)} %attn_state_ref.3) | copy-start | bytes 9220
  15.2 36.0 %collective-permute-start.1 = (bf16[576,768]{1,0:T(8,128)(2,1)S(1)}, bf16[576,768]{1,0:T(8,128)(2,1)S(1)}, u32[]{:S(2)}, u32[]{:S(2)}) collective-permute-start(bf16[576,768]{1,0:T(8,128)(2,1)S(1)} %get-tuple-element.49), channel_id=1, source_target_pairs={{0,128},{32,160},{64,192},{96,224},{128,0},{160,32},{192,64},{224,... | collective-permute-start | bytes 2654216 | tf_op jit(solution)/shard_map/ppermute | solution.py:349
  16.6 1.2 %collective-permute-start = (f32[1,1536]{1,0:T(1,128)S(1)}, f32[1,1536]{1,0:T(1,128)S(1)}, u32[]{:S(2)}, u32[]{:S(2)}) collective-permute-start(f32[1,1536]{1,0:T(1,128)S(1)} %get-tuple-element.36), channel_id=1, source_target_pairs={{0,1},{1,0},{2,3},{3,2},{4,5},{5,4},{6,7},{7,6},{8,9},{9,8},{10,11... | collective-permute-start | bytes 18440 | tf_op jit(solution)/shard_map/ppermute | solution.py:353
  48.0 13.2 %collective-permute-start.10 = (bf16[192,768]{1,0:T(8,128)(2,1)S(1)}, bf16[192,768]{1,0:T(8,128)(2,1)S(1)}, u32[]{:S(2)}, u32[]{:S(2)}) collective-permute-start(bf16[192,768]{1,0:T(8,128)(2,1)S(1)} %get-tuple-element.39.block_ref), channel_id=1, source_target_pairs={{0,192},{32,224},{64,128},{96,160},{128,64},{160,96},{192,0},{224,... | collective-permute-start | bytes 884744 | tf_op jit(solution)/shard_map/ppermute | solution.py:349
  49.1 13.4 %collective-permute-start.9 = (bf16[192,768]{1,0:T(8,128)(2,1)S(1)}, bf16[192,768]{1,0:T(8,128)(2,1)S(1)}, u32[]{:S(2)}, u32[]{:S(2)}) collective-permute-start(bf16[192,768]{1,0:T(8,128)(2,1)S(1)} %get-tuple-element.39.block_ref), channel_id=1, source_target_pairs={{0,64},{32,96},{64,0},{96,32},{128,192},{160,224},{192,128},{224,1... | collective-permute-start | bytes 884744 | tf_op jit(solution)/shard_map/ppermute | solution.py:349
  49.2 6.7 %collective-permute-start.3 = (bf16[96,768]{1,0:T(8,128)(2,1)S(1)}, bf16[96,768]{1,0:T(8,128)(2,1)S(1)}, u32[]{:S(2)}, u32[]{:S(2)}) collective-permute-start(bf16[96,768]{1,0:T(8,128)(2,1)S(1)} %get-tuple-element.50), channel_id=1, source_target_pairs={{0,32},{32,0},{64,96},{96,64},{128,160},{160,128},{192,224},{224,1... | collective-permute-start | bytes 442376 | tf_op jit(solution)/shard_map/ppermute | solution.py:349
  49.8 9.3 %collective-permute-start.6 = (bf16[96,768]{1,0:T(8,128)(2,1)S(1)}, bf16[96,768]{1,0:T(8,128)(2,1)S(1)}, u32[]{:S(2)}, u32[]{:S(2)}) collective-permute-start(bf16[96,768]{1,0:T(8,128)(2,1)S(1)} %get-tuple-element.51), channel_id=1, source_target_pairs={{0,32},{32,0},{64,96},{96,64},{128,160},{160,128},{192,224},{224,1... | collective-permute-start | bytes 442376 | tf_op jit(solution)/shard_map/ppermute | solution.py:349
  51.5 17.4 %collective-permute-start.2 = (bf16[192,768]{1,0:T(8,128)(2,1)S(1)}, bf16[192,768]{1,0:T(8,128)(2,1)S(1)}, u32[]{:S(2)}, u32[]{:S(2)}) collective-permute-start(bf16[192,768]{1,0:T(8,128)(2,1)S(1)} %shard_map.141.refs_0_), channel_id=1, source_target_pairs={{0,32},{32,0},{64,96},{96,64},{128,160},{160,128},{192,224},{224,1... | collective-permute-start | bytes 884744 | tf_op jit(solution)/shard_map/ppermute | solution.py:349
  55.9 10.7 %collective-permute-start.4 = (bf16[96,768]{1,0:T(8,128)(2,1)S(1)}, bf16[96,768]{1,0:T(8,128)(2,1)S(1)}, u32[]{:S(2)}, u32[]{:S(2)}) collective-permute-start(bf16[96,768]{1,0:T(8,128)(2,1)S(1)} %collective-permute-done.3.refs_1_), channel_id=1, source_target_pairs={{0,64},{32,96},{64,0},{96,32},{128,192},{160,224},{192,128},{224,1... | collective-permute-start | bytes 442376 | tf_op jit(solution)/shard_map/ppermute | solution.py:349
  59.1 7.5 %collective-permute-start.5 = (bf16[96,768]{1,0:T(8,128)(2,1)S(1)}, bf16[96,768]{1,0:T(8,128)(2,1)S(1)}, u32[]{:S(2)}, u32[]{:S(2)}) collective-permute-start(bf16[96,768]{1,0:T(8,128)(2,1)S(1)} %collective-permute-done.3.refs_1_), channel_id=1, source_target_pairs={{0,192},{32,224},{64,128},{96,160},{128,64},{160,96},{192,0},{224,... | collective-permute-start | bytes 442376 | tf_op jit(solution)/shard_map/ppermute | solution.py:349
  61.2 5.5 %collective-permute-start.7 = (bf16[96,768]{1,0:T(8,128)(2,1)S(1)}, bf16[96,768]{1,0:T(8,128)(2,1)S(1)}, u32[]{:S(2)}, u32[]{:S(2)}) collective-permute-start(bf16[96,768]{1,0:T(8,128)(2,1)S(1)} %collective-permute-done.6.refs_2_), channel_id=1, source_target_pairs={{0,64},{32,96},{64,0},{96,32},{128,192},{160,224},{192,128},{224,1... | collective-permute-start | bytes 442376 | tf_op jit(solution)/shard_map/ppermute | solution.py:349
  62.6 6.4 %collective-permute-start.8 = (bf16[96,768]{1,0:T(8,128)(2,1)S(1)}, bf16[96,768]{1,0:T(8,128)(2,1)S(1)}, u32[]{:S(2)}, u32[]{:S(2)}) collective-permute-start(bf16[96,768]{1,0:T(8,128)(2,1)S(1)} %collective-permute-done.6.refs_2_), channel_id=1, source_target_pairs={{0,192},{32,224},{64,128},{96,160},{128,64},{160,96},{192,0},{224,... | collective-permute-start | bytes 442376 | tf_op jit(solution)/shard_map/ppermute | solution.py:349

commit v3 on v2

--- a/solution.py
+++ b/solution.py
@@ -469,11 +469,8 @@
         ((2, 0, 0), (0, 1, 0), (0, 1, attn_cols // 2), (NEAR, 0, 0), (FAR, 0, 0)),
         (across, partner, partner_last, near, far),
     )
-    copy = fill(
-        copy,
-        ((2, 1, 0), (NEAR, 1, 0), (FAR, 1, 0), (NEAR, 1, attn_cols // 2), (FAR, 1, attn_cols // 2)),
-        (partner_across, partner_near, partner_far, last_near, last_far),
-    )
+    copy = fill(copy, ((2, 1, 0), (NEAR, 1, 0), (FAR, 1, 0)), (partner_across, partner_near, partner_far))
+    copy = fill(copy, ((NEAR, 1, attn_cols // 2), (FAR, 1, attn_cols // 2)), (last_near, last_far))
     return mlp_new, attn_new.T, rows_new, cols_new, attn_rows_new, attn_cols_new, copy.T
 
 

time: 70.1 us -> 69.9 us (level)
  waiting for transfers between devices: 8.4 us -> 7.53 us
    ppermute x10, waiting for transfers between devices: 7.24 us -> 6.36 us  [moved(): return lax.ppermute(value, ROW, pairs)]
    pallas_call x9 -> x10, Pallas kernels: 7.63 us -> 8.26 us  [call(): pl.pallas_call(kernel, out_shape=outs, in_specs=in_specs or [ON_CHIP] * l...]
  transfers between devices with their start and end apart: 11 -> 11, of which waited for: 4 -> 4; matrix products, arithmetic and copies ran while one was open for 0% -> 0% of each run, Pallas kernels for 5% -> 6%
where the time goes in v3:
time: 69.9 us; the launch traced here: 69.7 us
  blocking collectives  41.2 us (59%)
  starting transfers between devices  11.9 us (17%)
  Pallas kernels  8.26 us (12%)
  waiting for transfers between devices  7.53 us (11%)
  between operations  0.77 us (1%)
    all_to_all x3, blocking collectives, everyone(): return lax.all_to_all(value, axes, 0, 0, tiled=True)  41.2 us
    ppermute x10, starting transfers between devices, moved(): return lax.ppermute(value, ROW, pairs)  11.9 us
    pallas_call x10, Pallas kernels, call(): pl.pallas_call(kernel, out_shape=outs, in_specs=in_specs or [ON_CHIP] * l...  8.26 us
    ppermute x10, waiting for transfers between devices, moved(): return lax.ppermute(value, ROW, pairs)  6.36 us
  transfers between devices with their start and end apart: 11, of which 4 were waited for; matrix products, arithmetic and copies ran while one was open for 0% of the time, Pallas kernels for 6%

profile of v3, /device:TPU:32, one launch (start us, length us, event | category | flops | bytes accessed | tf_op | source)
XLA Modules:
  0.0 69.7 jit_solution(11245141887702830335)
XLA Ops:
  0.7 2.5 %shard_map.135 = (f32[8,1,1024]{2,1,0:T(1,128)S(1)}, f32[1,1536]{1,0:T(1,128)S(1)}, f32[1,256]{1,0:T(1,128)S(1)}, bf16[768,768]{1,0:T(8,128)(2,1)S(1)}, bf16[192...) custom-call(bf16[768,768]{1,0:T(8,128)(2,1)} %g_hbm.1, bf16[192,768]{1,0:T(8,128)(2,1)} %bitcast.6, ...), custom_call_target="tpu_custom_call" | custom-call | tf_op jit(solution)/shard_map/pallas_call | solution.py:30
  3.1 0.0 copy-start.1
  3.2 0.0 copy-start.2
  3.2 11.3 %all_to_all.15.got_ref = f32[8,1,1024]{2,1,0:T(1,128)S(1)} all-to-all(f32[8,1,1024]{2,1,0:T(1,128)S(1)} %get-tuple-element.30), channel_id=1, replica_groups=mesh['row_0'=4,'row_1'=2,'col_0'=2,'col_1'=8,'col_2'=2] {'row_0','row_1'}, dimensions={0} | all-to-all | bytes 65536 | tf_op jit(solution)/shard_map/all_to_all | solution.py:342
  14.5 0.7 %shard_map.136 = (f32[768]{0:T(1024)S(1)}, f32[192]{0:T(256)S(1)}, f32[1,1536]{1,0:T(1,128)S(1)}, f32[1,1536]{1,0:T(1,128)S(1)}, bf16[576,768]{1,0:T(8,128)(2,1)S(1)}) custom-call(f32[8,1,1024]{2,1,0:T(1,128)S(1)} %all_to_all.15.got_ref, f32[1,1536]{1,0:T(1,128)S(1)} %get-tuple-element.31.rows_ref, bf16[768,768]{1,0:T(8,128)(2,1)S(1)} %get-tuple-element.32.g_ref, ...), custom_call_target="tpu_custom_call" | custom-call | tf_op jit(solution)/shard_map/pallas_call | solution.py:30
  15.2 1.3 %collective-permute-start.4 = (bf16[576,768]{1,0:T(8,128)(2,1)S(1)}, bf16[576,768]{1,0:T(8,128)(2,1)S(1)}, u32[]{:S(2)}, u32[]{:S(2)}) collective-permute-start(bf16[576,768]{1,0:T(8,128)(2,1)S(1)} %get-tuple-element.50), channel_id=1, source_target_pairs={{0,128},{32,160},{64,192},{96,224},{128,0},{160,32},{192,64},{224,... | collective-permute-start | bytes 2654216 | tf_op jit(solution)/shard_map/ppermute | solution.py:349
  16.6 0.0 collective-permute-start
  16.6 1.2 %collective-permute-done.got_ref = f32[1,1536]{1,0:T(1,128)S(1)} collective-permute-done((f32[1,1536]{1,0:T(1,128)S(1)}, f32[1,1536]{1,0:T(1,128)S(1)}, u32[]{:S(2)}, u32[]{:S(2)}) %collective-permute-start) | collective-permute-done | bytes 6176 | tf_op jit(solution)/shard_map/ppermute | solution.py:353
  17.8 20.2 %all_to_all.16.got_ref = f32[16,1,1792]{2,1,0:T(1,128)S(1)} all-to-all(f32[16,1,1792]{2,1,0:T(1,128)S(1)} %shard_map.137), channel_id=1, replica_groups=mesh['row_0'=4,'row_1'=2,'col_0'=2,'col_1'=8,'col_2'=2] {'col_0','col_1'}, dimensions={0} | all-to-all | bytes 229376 | tf_op jit(solution)/shard_map/all_to_all | solution.py:342
  38.0 9.6 %all_to_all.17.got_ref = f32[16,1,1280]{2,1,0:T(1,128)S(1)} all-to-all(f32[16,1,1280]{2,1,0:T(1,128)S(1)} %shard_map.138), channel_id=1, replica_groups=mesh['row_0'=4,'row_1'=2,'col_0'=2,'col_1'=8,'col_2'=2] {'row_0','row_1'..., dimensions={0} | all-to-all | bytes 163840 | tf_op jit(solution)/shard_map/all_to_all | solution.py:342
  47.7 0.3 shard_map.139
  48.0 1.2 %collective-permute-start.10 = (bf16[192,768]{1,0:T(8,128)(2,1)S(1)}, bf16[192,768]{1,0:T(8,128)(2,1)S(1)}, u32[]{:S(2)}, u32[]{:S(2)}) collective-permute-start(bf16[192,768]{1,0:T(8,128)(2,1)S(1)} %get-tuple-element.39.block_ref), channel_id=1, source_target_pairs={{0,192},{32,224},{64,128},{96,160},{128,64},{160,96},{192,0},{224,... | collective-permute-start | bytes 884744 | tf_op jit(solution)/shard_map/ppermute | solution.py:349
  49.2 0.1 collective-permute-start.9
  49.2 0.6 collective-permute-start.6
  49.8 1.4 %collective-permute-start.1 = (bf16[96,768]{1,0:T(8,128)(2,1)S(1)}, bf16[96,768]{1,0:T(8,128)(2,1)S(1)}, u32[]{:S(2)}, u32[]{:S(2)}) collective-permute-start(bf16[96,768]{1,0:T(8,128)(2,1)S(1)} %get-tuple-element.49), channel_id=1, source_target_pairs={{0,32},{32,0},{64,96},{96,64},{128,160},{160,128},{192,224},{224,1... | collective-permute-start | bytes 442376 | tf_op jit(solution)/shard_map/ppermute | solution.py:349
  51.2 0.0 collective-permute-done.4.ahead_ref
  51.3 0.3 shard_map.141.refs_0_
  51.5 0.7 %collective-permute-start.5 = (bf16[192,768]{1,0:T(8,128)(2,1)S(1)}, bf16[192,768]{1,0:T(8,128)(2,1)S(1)}, u32[]{:S(2)}, u32[]{:S(2)}) collective-permute-start(bf16[192,768]{1,0:T(8,128)(2,1)S(1)} %shard_map.141.refs_0_), channel_id=1, source_target_pairs={{0,32},{32,0},{64,96},{96,64},{128,160},{160,128},{192,224},{224,1... | collective-permute-start | bytes 884744 | tf_op jit(solution)/shard_map/ppermute | solution.py:349
  52.2 3.7 %collective-permute-done.6.refs_1_ = bf16[96,768]{1,0:T(8,128)(2,1)S(1)} collective-permute-done((bf16[96,768]{1,0:T(8,128)(2,1)S(1)}, bf16[96,768]{1,0:T(8,128)(2,1)S(1)}, u32[]{:S(2)}, u32[]{:S(2)}) %collective-permute-start.6) | collective-permute-done | bytes 147488 | tf_op jit(solution)/shard_map/ppermute | solution.py:349
  55.9 2.0 %collective-permute-start.7 = (bf16[96,768]{1,0:T(8,128)(2,1)S(1)}, bf16[96,768]{1,0:T(8,128)(2,1)S(1)}, u32[]{:S(2)}, u32[]{:S(2)}) collective-permute-start(bf16[96,768]{1,0:T(8,128)(2,1)S(1)} %collective-permute-done.6.refs_1_), channel_id=1, source_target_pairs={{0,64},{32,96},{64,0},{96,32},{128,192},{160,224},{192,128},{224,1... | collective-permute-start | bytes 442376 | tf_op jit(solution)/shard_map/ppermute | solution.py:349
  57.9 1.2 %collective-permute-done.1.refs_2_ = bf16[96,768]{1,0:T(8,128)(2,1)S(1)} collective-permute-done((bf16[96,768]{1,0:T(8,128)(2,1)S(1)}, bf16[96,768]{1,0:T(8,128)(2,1)S(1)}, u32[]{:S(2)}, u32[]{:S(2)}) %collective-permute-start.1) | collective-permute-done | bytes 147488 | tf_op jit(solution)/shard_map/ppermute | solution.py:349
  59.1 2.1 %collective-permute-start.8 = (bf16[96,768]{1,0:T(8,128)(2,1)S(1)}, bf16[96,768]{1,0:T(8,128)(2,1)S(1)}, u32[]{:S(2)}, u32[]{:S(2)}) collective-permute-start(bf16[96,768]{1,0:T(8,128)(2,1)S(1)} %collective-permute-done.6.refs_1_), channel_id=1, source_target_pairs={{0,192},{32,224},{64,128},{96,160},{128,64},{160,96},{192,0},{224,... | collective-permute-start | bytes 442376 | tf_op jit(solution)/shard_map/ppermute | solution.py:349
  61.2 0.0 collective-permute-done.10.refs_4_
  61.2 1.4 %collective-permute-start.2 = (bf16[96,768]{1,0:T(8,128)(2,1)S(1)}, bf16[96,768]{1,0:T(8,128)(2,1)S(1)}, u32[]{:S(2)}, u32[]{:S(2)}) collective-permute-start(bf16[96,768]{1,0:T(8,128)(2,1)S(1)} %collective-permute-done.1.refs_2_), channel_id=1, source_target_pairs={{0,64},{32,96},{64,0},{96,32},{128,192},{160,224},{192,128},{224,1... | collective-permute-start | bytes 442376 | tf_op jit(solution)/shard_map/ppermute | solution.py:349
  62.6 1.1 %collective-permute-start.3 = (bf16[96,768]{1,0:T(8,128)(2,1)S(1)}, bf16[96,768]{1,0:T(8,128)(2,1)S(1)}, u32[]{:S(2)}, u32[]{:S(2)}) collective-permute-start(bf16[96,768]{1,0:T(8,128)(2,1)S(1)} %collective-permute-done.1.refs_2_), channel_id=1, source_target_pairs={{0,192},{32,224},{64,128},{96,160},{128,64},{160,96},{192,0},{224,... | collective-permute-start | bytes 442376 | tf_op jit(solution)/shard_map/ppermute | solution.py:349
  63.7 1.8 %shard_map.140 = (bf16[192,6144]{1,0:T(8,128)(2,1)}, f32[192,768]{1,0:T(8,128)}, f32[768,768]{1,0:T(8,128)}, f32[768]{0:T(1024)}, f32[768]{0:T(1024)}, /*index=5*/f32[768]{0:T(1024)}, f32[192]{0:T(256)}) custom-call(bf16[192,768]{1,0:T(8,128)(2,1)S(1)} %get-tuple-element.39.block_ref, f32[16,1,1280]{2,1,0:T(1,128)S(1)} %all_to_all.17.got_ref, ...), custom_call_target="tpu_custom_call" | custom-call | flops 4194304 | bytes 4194304 | tf_op jit(solution)/shard_map/pallas_call | solution.py:30
  65.5 1.1 %shard_map.142.refs_3_ = bf16[192,6144]{1,0:T(8,128)(2,1)} custom-call(bf16[192,768]{1,0:T(8,128)(2,1)S(1)} %shard_map.141.refs_0_, bf16[96,768]{1,0:T(8,128)(2,1)S(1)} %collective-permute-done.6.refs_1_, bf16[96,768]{1,0:T(8,128)(2,1)S(1)} %collective-permute-done.1.refs_2_, ...), custom_call_target="tpu_custom_call", output_to_operand_aliasing={{}: (5, {})} | custom-call | tf_op jit(solution)/shard_map/pallas_call | solution.py:30
  66.6 0.0 collective-permute-done.7.refs_1_
  66.6 0.0 collective-permute-done.5.refs_0_
  66.6 0.9 %shard_map.143.refs_2_ = bf16[192,6144]{1,0:T(8,128)(2,1)} custom-call(bf16[192,768]{1,0:T(8,128)(2,1)S(1)} %collective-permute-done.5.refs_0_, bf16[96,768]{1,0:T(8,128)(2,1)S(1)} %collective-permute-done.7.refs_1_, bf16[96,768]{1,0:T(8,128)(2,1)S(1)} %collective-permute-done.8.refs_2_, ...), custom_call_target="tpu_custom_call", output_to_operand_aliasing={{}: (3, {})} | custom-call | tf_op jit(solution)/shard_map/pallas_call | solution.py:30
  67.5 1.4 %collective-permute-done.3.refs_1_ = bf16[96,768]{1,0:T(8,128)(2,1)S(1)} collective-permute-done((bf16[96,768]{1,0:T(8,128)(2,1)S(1)}, bf16[96,768]{1,0:T(8,128)(2,1)S(1)}, u32[]{:S(2)}, u32[]{:S(2)}) %collective-permute-start.3) | collective-permute-done | bytes 147488 | tf_op jit(solution)/shard_map/ppermute | solution.py:349
  68.9 0.7 %shard_map.144 = bf16[192,6144]{1,0:T(8,128)(2,1)} custom-call(bf16[96,768]{1,0:T(8,128)(2,1)S(1)} %collective-permute-done.2.refs_0_, bf16[96,768]{1,0:T(8,128)(2,1)S(1)} %collective-permute-done.3.refs_1_, bf16[192,6144]{1,0:T(8,128)(2,1)} %shard_map.143.refs_2_), custom_call_target="tpu_custom_call", output_to_operand_aliasing={{}: (2, {})} | custom-call | tf_op jit(solution)/shard_map/pallas_call | solution.py:30
  (11 shorter events, 0.1 us)
Async XLA Ops:
  0.6 13.9 %copy-start = (f32[768]{0:T(1024)S(1)}, f32[768]{0:T(1024)}, u32[]{:S(2)}) copy-start(f32[768]{0:T(1024)} %state_ref.2) | copy-start | bytes 9220
  0.6 13.9 %copy-start.3 = (f32[192]{0:T(256)S(1)}, f32[192]{0:T(256)}, u32[]{:S(2)}) copy-start(f32[192]{0:T(256)} %attn_state_ref.2) | copy-start | bytes 2308
  3.1 34.8 %copy-start.1 = (f32[768]{0:T(1024)S(1)}, f32[768]{0:T(1024)}, u32[]{:S(2)}) copy-start(f32[768]{0:T(1024)} %state_ref.3) | copy-start | bytes 9220
  3.2 34.8 %copy-start.2 = (f32[768]{0:T(1024)S(1)}, f32[768]{0:T(1024)}, u32[]{:S(2)}) copy-start(f32[768]{0:T(1024)} %attn_state_ref.3) | copy-start | bytes 9220
  15.2 36.0 %collective-permute-start.4 = (bf16[576,768]{1,0:T(8,128)(2,1)S(1)}, bf16[576,768]{1,0:T(8,128)(2,1)S(1)}, u32[]{:S(2)}, u32[]{:S(2)}) collective-permute-start(bf16[576,768]{1,0:T(8,128)(2,1)S(1)} %get-tuple-element.50), channel_id=1, source_target_pairs={{0,128},{32,160},{64,192},{96,224},{128,0},{160,32},{192,64},{224,... | collective-permute-start | bytes 2654216 | tf_op jit(solution)/shard_map/ppermute | solution.py:349
  16.6 1.2 %collective-permute-start = (f32[1,1536]{1,0:T(1,128)S(1)}, f32[1,1536]{1,0:T(1,128)S(1)}, u32[]{:S(2)}, u32[]{:S(2)}) collective-permute-start(f32[1,1536]{1,0:T(1,128)S(1)} %get-tuple-element.36), channel_id=1, source_target_pairs={{0,1},{1,0},{2,3},{3,2},{4,5},{5,4},{6,7},{7,6},{8,9},{9,8},{10,11... | collective-permute-start | bytes 18440 | tf_op jit(solution)/shard_map/ppermute | solution.py:353
  48.0 13.2 %collective-permute-start.10 = (bf16[192,768]{1,0:T(8,128)(2,1)S(1)}, bf16[192,768]{1,0:T(8,128)(2,1)S(1)}, u32[]{:S(2)}, u32[]{:S(2)}) collective-permute-start(bf16[192,768]{1,0:T(8,128)(2,1)S(1)} %get-tuple-element.39.block_ref), channel_id=1, source_target_pairs={{0,192},{32,224},{64,128},{96,160},{128,64},{160,96},{192,0},{224,... | collective-permute-start | bytes 884744 | tf_op jit(solution)/shard_map/ppermute | solution.py:349
  49.2 13.4 %collective-permute-start.9 = (bf16[192,768]{1,0:T(8,128)(2,1)S(1)}, bf16[192,768]{1,0:T(8,128)(2,1)S(1)}, u32[]{:S(2)}, u32[]{:S(2)}) collective-permute-start(bf16[192,768]{1,0:T(8,128)(2,1)S(1)} %get-tuple-element.39.block_ref), channel_id=1, source_target_pairs={{0,64},{32,96},{64,0},{96,32},{128,192},{160,224},{192,128},{224,1... | collective-permute-start | bytes 884744 | tf_op jit(solution)/shard_map/ppermute | solution.py:349
  49.2 6.7 %collective-permute-start.6 = (bf16[96,768]{1,0:T(8,128)(2,1)S(1)}, bf16[96,768]{1,0:T(8,128)(2,1)S(1)}, u32[]{:S(2)}, u32[]{:S(2)}) collective-permute-start(bf16[96,768]{1,0:T(8,128)(2,1)S(1)} %get-tuple-element.51), channel_id=1, source_target_pairs={{0,32},{32,0},{64,96},{96,64},{128,160},{160,128},{192,224},{224,1... | collective-permute-start | bytes 442376 | tf_op jit(solution)/shard_map/ppermute | solution.py:349
  49.8 9.3 %collective-permute-start.1 = (bf16[96,768]{1,0:T(8,128)(2,1)S(1)}, bf16[96,768]{1,0:T(8,128)(2,1)S(1)}, u32[]{:S(2)}, u32[]{:S(2)}) collective-permute-start(bf16[96,768]{1,0:T(8,128)(2,1)S(1)} %get-tuple-element.49), channel_id=1, source_target_pairs={{0,32},{32,0},{64,96},{96,64},{128,160},{160,128},{192,224},{224,1... | collective-permute-start | bytes 442376 | tf_op jit(solution)/shard_map/ppermute | solution.py:349
  51.5 15.1 %collective-permute-start.5 = (bf16[192,768]{1,0:T(8,128)(2,1)S(1)}, bf16[192,768]{1,0:T(8,128)(2,1)S(1)}, u32[]{:S(2)}, u32[]{:S(2)}) collective-permute-start(bf16[192,768]{1,0:T(8,128)(2,1)S(1)} %shard_map.141.refs_0_), channel_id=1, source_target_pairs={{0,32},{32,0},{64,96},{96,64},{128,160},{160,128},{192,224},{224,1... | collective-permute-start | bytes 884744 | tf_op jit(solution)/shard_map/ppermute | solution.py:349
  55.9 10.7 %collective-permute-start.7 = (bf16[96,768]{1,0:T(8,128)(2,1)S(1)}, bf16[96,768]{1,0:T(8,128)(2,1)S(1)}, u32[]{:S(2)}, u32[]{:S(2)}) collective-permute-start(bf16[96,768]{1,0:T(8,128)(2,1)S(1)} %collective-permute-done.6.refs_1_), channel_id=1, source_target_pairs={{0,64},{32,96},{64,0},{96,32},{128,192},{160,224},{192,128},{224,1... | collective-permute-start | bytes 442376 | tf_op jit(solution)/shard_map/ppermute | solution.py:349
  59.1 7.5 %collective-permute-start.8 = (bf16[96,768]{1,0:T(8,128)(2,1)S(1)}, bf16[96,768]{1,0:T(8,128)(2,1)S(1)}, u32[]{:S(2)}, u32[]{:S(2)}) collective-permute-start(bf16[96,768]{1,0:T(8,128)(2,1)S(1)} %collective-permute-done.6.refs_1_), channel_id=1, source_target_pairs={{0,192},{32,224},{64,128},{96,160},{128,64},{160,96},{192,0},{224,... | collective-permute-start | bytes 442376 | tf_op jit(solution)/shard_map/ppermute | solution.py:349
  61.2 6.3 %collective-permute-start.2 = (bf16[96,768]{1,0:T(8,128)(2,1)S(1)}, bf16[96,768]{1,0:T(8,128)(2,1)S(1)}, u32[]{:S(2)}, u32[]{:S(2)}) collective-permute-start(bf16[96,768]{1,0:T(8,128)(2,1)S(1)} %collective-permute-done.1.refs_2_), channel_id=1, source_target_pairs={{0,64},{32,96},{64,0},{96,32},{128,192},{160,224},{192,128},{224,1... | collective-permute-start | bytes 442376 | tf_op jit(solution)/shard_map/ppermute | solution.py:349
  62.6 6.4 %collective-permute-start.3 = (bf16[96,768]{1,0:T(8,128)(2,1)S(1)}, bf16[96,768]{1,0:T(8,128)(2,1)S(1)}, u32[]{:S(2)}, u32[]{:S(2)}) collective-permute-start(bf16[96,768]{1,0:T(8,128)(2,1)S(1)} %collective-permute-done.1.refs_2_), channel_id=1, source_target_pairs={{0,192},{32,224},{64,128},{96,160},{128,64},{160,96},{192,0},{224,... | collective-permute-start | bytes 442376 | tf_op jit(solution)/shard_map/ppermute | solution.py:349
